TPU v7x, 32 devices: a whole 2x2x4 slice. The times are simulated.
32 devices in a mesh: rows: 32 (over z, y, x, core).
Axes of the slice: x: 2, y: 2, z: 4, core: 2. Of those that a mesh axis runs over, the one named last changes fastest.
Arguments:
- source: float32 [128, 2048], P('rows'), may hold values from -60 to 60
- observed: float32 [128, 2048], P('rows'), may hold values from -4 to 4
- precision: float32 [128, 2048], P('rows'), may hold values from 1 to 10
- conductivity: float32 [128, 2048], P('rows'), may hold values from 0.5 to 2
- log_field: float32 [16, 128, 2048], P(None, 'rows'), may hold values from -4 to 4
- noise_field: float32 [16, 128, 2048], P(None, 'rows'), may hold values from -6 to 6
- subspace_noise: float32 [16, 256], replicated, may hold values from -6 to 6
- eigenvalues: float32 [256], replicated, may hold values from 0.1 to 100
- basis: bfloat16 [256, 128, 2048], P(None, 'rows'), may hold values from -0.0234375 to 0.0234375
Outputs:
- proposal: float32 [16, 128, 2048], P(None, 'rows')
- new_coef: float32 [16, 256], replicated
All inputs are finite; a program needn't handle non-finite values.
Results may differ from a plain program's by a relative error of at most 0.0003.
The roundings to bfloat16 on the way count: a program that leaves them out, or rounds other values in their place, can miss the bound.
Values sent between devices are 32-bit elements; how exact they have to be, the bound alone decides.
No kernel may reach another device: no remote copies, remote signals or barrier semaphores. Data moves between devices by JAX's collectives and lax.ppermute only.
A program may use at most 64 MiB of HBM per device.

v0:
```python
import functools
import math

import jax
import jax.numpy as jnp
from jax import lax
from jax.experimental import pallas as pl
from jax.experimental.pallas import tpu as pltpu
from jax.sharding import PartitionSpec as P

ITERS = 4
SHIFTS = (0.0, 0.5, 1.0)
AXIS = "rows"
SUB, LANES = 8, 128
SUMS = 2 * ITERS * len(SHIFTS)


def shifted(value, step):
    count = lax.axis_size(AXIS)
    pairs = [(i, i + step) for i in range(count) if 0 <= i + step < count]
    return lax.ppermute(value, AXIS, pairs)


def exchanged(value):
    return lax.all_to_all(value, AXIS, 0, 0)


def summed(value):
    count = lax.axis_size(AXIS)
    if count & (count - 1):
        return lax.psum(value, AXIS)
    stride = 1
    while stride < count:
        radix = 4 if (count // stride).bit_length() & 1 else 2
        parts = [value]
        for k in range(1, radix):
            parts.append(lax.ppermute(value, AXIS, [(i, i ^ (k * stride)) for i in range(count)]))
        while len(parts) > 1:
            parts = [a + b for a, b in zip(parts[::2], parts[1::2])]
        value = parts[0]
        stride *= radix
    return value


def differences(sequence, shift):
    out = [sequence[0]]
    while len(sequence) > 1:
        if shift == 0.0:
            sequence = sequence[1:]
        elif shift == 1.0:
            sequence = [b - a for a, b in zip(sequence[:-1], sequence[1:])]
        else:
            sequence = [b - shift * a for a, b in zip(sequence[:-1], sequence[1:])]
        out.append(sequence[0])
    return out


def coefficients(sums):
    chosen, best = None, None
    for index, shift in enumerate(SHIFTS):
        eta = sums[index * 2 * ITERS : (index + 1) * 2 * ITERS]
        gram = [(1.0 - shift) * eta[k] - eta[k + 1] for k in range(2 * ITERS - 1)]
        low = [[None] * ITERS for _ in range(ITERS)]
        scaled = [[None] * ITERS for _ in range(ITERS)]
        inverse, reduced, quality = [None] * ITERS, [None] * ITERS, None
        for i in range(ITERS):
            for j in range(i):
                entry = gram[i + j]
                for k in range(j):
                    entry = entry - low[i][k] * scaled[j][k]
                scaled[i][j] = entry
                low[i][j] = entry * inverse[j]
            pivot, target = gram[2 * i], eta[i]
            for k in range(i):
                pivot = pivot - low[i][k] * scaled[i][k]
                target = target - low[i][k] * reduced[k]
            size = (1.0 - shift) * eta[2 * i] + jnp.abs(eta[2 * i + 1])
            usable = pivot > 1e-6 * gram[2 * i]
            ratio = jnp.where(usable, pivot, 0.0) / jnp.where(size > 0.0, size, 1.0)
            quality = ratio if quality is None else jnp.minimum(quality, ratio)
            inverse[i] = jnp.where(usable, 1.0 / jnp.where(usable, pivot, 1.0), 0.0)
            reduced[i] = target
        weights = [None] * ITERS
        for i in reversed(range(ITERS)):
            entry = reduced[i] * inverse[i]
            for k in range(i + 1, ITERS):
                entry = entry - low[k][i] * weights[k]
            weights[i] = entry
        if shift != 0.0:
            for step in range(ITERS - 1):
                for k in range(ITERS - 2, step - 1, -1):
                    weights[k] = weights[k] - shift * weights[k + 1]
        if chosen is None:
            chosen, best = weights, quality
        else:
            better = quality > best
            chosen = [jnp.where(better, a, b) for a, b in zip(weights, chosen)]
            best = jnp.where(better, quality, best)
    return chosen


def krylov(vectors, images, inverse, across, along):
    width = across.shape[-1]
    groups = inverse.shape[1]
    for k in range(ITERS - 1):
        for i in range(images[k].shape[0]):
            at = i + k + 1
            for g in range(groups):
                v = vectors[k][i + 1, g]
                side = across[at]
                beside = pltpu.roll(side * v, 1, 1) + side * pltpu.roll(v, width - 1, 1)
                image = along[at] * vectors[k][i, g] + along[at + 1] * vectors[k][i + 2, g] + beside
                images[k][i, g] = image
                vectors[k + 1][i, g] = image * inverse[at, g]


def moment_tile(rows, right_side, vectors, images, thirds, halves, across, along):
    width = across.shape[-1]
    groups = vectors[0].shape[1]
    above = ITERS - 1
    for index, shift in enumerate(SHIFTS):
        for g in range(groups):
            for r in range(rows + 1):
                v = [vectors[k][r + above - k, g] for k in range(ITERS)]
                thirds[index, r, g] = differences(v, shift)[ITERS - 1]
            for r in range(rows):
                u = pltpu.roll(thirds[index, r, g], width - 1, 1)
                u = across[above + r] * u + along[above + r + 1] * thirds[index, r + 1, g]
                halves[index, r, g] = u
    lane = lax.broadcasted_iota(jnp.int32, (SUB, LANES), 1)
    tile = jnp.zeros((SUB, LANES), jnp.float32)
    for g in range(groups):

        def one_row(r, totals):
            totals = list(totals)
            for start in range(0, width, LANES):
                cut = pl.ds(start, LANES)
                v = [vectors[k][r + above - k, g, :, cut] for k in range(ITERS - 1)]
                s = [right_side(r, g, cut)]
                s += [images[k][r + above - k - 1, g, :, cut] for k in range(ITERS - 1)]
                for index, shift in enumerate(SHIFTS):
                    u, t = differences(v, shift), differences(s, shift)
                    u.append(thirds[index, r, g, :, cut])
                    t.append(halves[index, r, g, :, cut])
                    for m in range(2 * ITERS):
                        slot = index * 2 * ITERS + m
                        totals[slot] = totals[slot] + u[m // 2] * t[(m + 1) // 2]
            return tuple(totals)

        zero = jnp.zeros((SUB, LANES), jnp.float32)
        totals = list(lax.fori_loop(0, rows, one_row, (zero,) * SUMS))
        for index, shift in enumerate(SHIFTS):
            last = (index + 1) * 2 * ITERS - 1
            totals[last] = 2.0 * totals[last] - shift * totals[last - 1]
        for m, total in enumerate(totals):
            tile = jnp.where(lane == g * SUMS + m, jnp.sum(total, 1, keepdims=True), tile)
    return (tile + pltpu.roll(pltpu.roll(tile, LANES // 2, 1), SUB // 2, 0))[: SUB // 2]


def spread(ref, at):
    return jnp.broadcast_to(ref[at : at + 1, :], (SUB, ref.shape[-1]))


def lateral(here):
    width = here.shape[-1]
    column = lax.broadcasted_iota(jnp.int32, here.shape, 1)
    left = jnp.where(column == 0, here, pltpu.roll(here, 1, 1))
    right = jnp.where(column == width - 1, here, pltpu.roll(here, width - 1, 1))
    right = 0.5 * (here + right)
    return 0.5 * (here + left), right, jnp.where(column == width - 1, 0.0, right)


class Packed:
    def __init__(self, rows, chains):
        self.rows, self.chains = rows, chains
        self.split = (rows - 2) * chains
        self.upward = self.split
        self.downward = (rows - 1) * chains + 2 * rows

    def log(self, row, g):
        at = row * self.chains + g * SUB
        return at if row < self.rows - 2 else at + 2 * self.rows

    def source(self, row):
        return self.split + row

    def cond(self, row):
        return self.split + self.rows + row


def forward_kernel(
    _,
    place,
    own,
    before,
    after,
    far,
    sent,
    v0,
    v1,
    v2,
    v3,
    inverse,
    across,
    along,
    cond,
    side,
    thirds,
    halves,
    *images,
    rows,
    groups,
):
    halo = ITERS
    above = halo - 1
    total = rows + above + halo
    spot = Packed(rows, groups * SUB)
    vectors = (v0, v1, v2, v3)
    first, last = place[0], place[1]
    for i in range(halo):
        at = spot.cond(rows - halo + i)
        cond[i] = jnp.where(first == 0, spread(own, spot.cond(0)), spread(before, at))
        at = spot.cond(i)
        cond[halo + rows + i] = jnp.where(
            last == 0, spread(own, spot.cond(rows - 1)), spread(after, at)
        )
    for i in range(rows):
        cond[halo + i] = spread(own, spot.cond(i))
    cond[total + 1] = jnp.where(last == 1, spread(after, spot.cond(halo - 1)), spread(far, 0))
    for i in range(total + 1):
        along[i] = 0.5 * (cond[i] + cond[i + 1])
    for i in range(total):
        left, right, across[i] = lateral(cond[i + 1])
        edges = along[i] + along[i + 1] + left + right
        if i < above:
            ref, row, outside = before, rows - above + i, first == 0
        elif i < above + rows:
            ref, row, outside = own, i - above, None
        else:
            ref, row, outside = after, i - above - rows, last == 0
        source = spread(ref, spot.source(row))
        if ref is own:
            side[row] = source
        for g in range(groups):
            start = spot.log(row, g)
            value = 1.0 / (edges + jnp.exp(ref[start : start + SUB, :]))
            if outside is not None:
                value = jnp.where(outside, 0.0, value)
            inverse[i, g] = value
            vectors[0][i, g] = source * value
    krylov(vectors, images, inverse, across, along)
    tile = moment_tile(
        rows, lambda r, g, cut: side[r, :, cut], vectors, images, thirds, halves, across, along
    )
    sent[...] = jnp.broadcast_to(tile[None], sent.shape)


def total_of(got):
    parts = [got[d] for d in range(got.shape[0])]
    while len(parts) > 1:
        parts = [a + b for a, b in zip(parts[::2], parts[1::2])] + parts[len(parts) & ~1 :]
    return jnp.concatenate([parts[0], pltpu.roll(parts[0], LANES // 2, 1)], 0)


def weights_of(tile, g):
    sums = [
        jnp.broadcast_to(tile[:, g * SUMS + m : g * SUMS + m + 1], (SUB, LANES)) for m in range(SUMS)
    ]
    return [weight[:, :1] for weight in coefficients(sums)]


def adjoint_kernel(
    place,
    got,
    f0,
    f1,
    f2,
    f3,
    inverse,
    across,
    along,
    before,
    after,
    far_before,
    far_after,
    precision,
    observed,
    sent,
    kept,
    state,
    side,
    outer,
    outer_inverse,
    outer_across,
    outer_along,
    thirds,
    halves,
    *scratch,
    rows,
    groups,
):
    halo = ITERS
    above = halo - 1
    width = across.shape[-1]
    chains = groups * SUB
    spot = Packed(rows, chains)
    first, last = place[0], place[1]
    near = (f0, f1, f2, f3)
    low, high = -above, rows + halo - 1
    new_rows = [low - k for k in (3, 2, 1)] + [high + k for k in (1, 2, 3)]
    slot = {row: i for i, row in enumerate(new_rows)}

    def cond_at(row):
        if row < -rows:
            at = row + 2 * rows
            value = spread(far_before, rows + at)
            return jnp.where(first == 1, spread(before, spot.cond(0)), value) if at == rows - 1 else value
        if row < 0:
            return spread(before, spot.cond(row + rows))
        if row < 2 * rows:
            return spread(after, spot.cond(row - rows))
        return spread(far_after, spot.cond(row - 2 * rows))

    for edge in range(low - 3, low):
        outer_along[edge - low + 3] = 0.5 * (cond_at(edge - 1) + cond_at(edge))
    for edge in range(high + 2, high + 5):
        outer_along[edge - high + 1] = 0.5 * (cond_at(edge - 1) + cond_at(edge))

    def along_at(row):
        if row < low:
            return outer_along[row - low + 3]
        if row > high + 1:
            return outer_along[row - high + 1]
        return along[row - low]

    def across_at(row):
        return outer_across[slot[row]] if row in slot else across[row - low]

    def inverse_at(row, g):
        return outer_inverse[slot[row], g] if row in slot else inverse[row - low, g]

    for row in new_rows:
        left, right, outer_across[slot[row]] = lateral(cond_at(row))
        edges = along_at(row) + along_at(row + 1) + left + right
        for g in range(groups):
            if row < -rows:
                at = row + 2 * rows
                outside, source = first <= 1, spread(far_before, at)
                start = 2 * rows + (at - rows + 2) * chains + g * SUB
                log = far_before[start : start + SUB, :]
            elif row < 0:
                outside, source = first == 0, spread(before, spot.source(row + rows))
                start = spot.log(row + rows, g)
                log = before[start : start + SUB, :]
            else:
                at = row - 2 * rows
                outside, source = last <= 1, spread(far_after, spot.source(at))
                start = spot.log(at, g)
                log = far_after[start : start + SUB, :]
            value = jnp.where(outside, 0.0, 1.0 / (edges + jnp.exp(log)))
            outer_inverse[slot[row], g] = value
            outer[0, slot[row], g] = source * value

    def vector(k, row, g):
        if row < low + k:
            return outer[k, row - low + 3 - k, g]
        if row > high - k:
            return outer[k, row - high + 2 + k, g]
        return near[k][row - low - k, g]

    for k in range(ITERS - 1):
        for i, row in enumerate([low + k + 1 - j for j in (3, 2, 1)] + [high - k - 1 + j for j in (1, 2, 3)]):
            for g in range(groups):
                v, edge = vector(k, row, g), across_at(row)
                image = pltpu.roll(edge * v, 1, 1) + edge * pltpu.roll(v, width - 1, 1)
                image = along_at(row) * vector(k, row - 1, g) + along_at(row + 1) * vector(k, row + 1, g) + image
                outer[k + 1, i, g] = image * inverse_at(row, g)

    vectors, images = scratch[:ITERS], scratch[ITERS:]
    tile = total_of(got)
    for g in range(groups):
        weights = weights_of(tile, g)
        for i in range(high - low + 1):
            row = low + i
            value = weights[0] * vector(0, row, g)
            for k in range(1, ITERS):
                value = value + weights[k] * vector(k, row, g)
            if row < 0:
                at = row + rows
                at = far_before.shape[0] - 2 * rows + at
                scale, target = spread(far_before, at), spread(far_before, at + rows)
            elif row < rows:
                state[row, g] = value
                scale, target = spread(precision, row), spread(observed, row)
            else:
                at = far_after.shape[0] - 2 * rows + row - rows
                scale, target = spread(far_after, at), spread(far_after, at + rows)
            value = scale * (value - target)
            if 0 <= row < rows:
                side[row, g] = value
            vectors[0][i, g] = value * inverse[i, g]
    krylov(vectors, images, inverse, across, along)
    tile = moment_tile(
        rows, lambda r, g, cut: side[r, g, :, cut], vectors, images, thirds, halves, across, along
    )
    sent[...] = jnp.broadcast_to(tile[None], sent.shape)
    for k in range(ITERS):
        for r in range(rows):
            for g in range(groups):
                kept[k, r, g] = vectors[k][r + above - k, g]


def factors(eigenvalues):
    variance = 1.0 / (1.0 + eigenvalues)
    below = 2.0 + 0.8 * variance
    return (2.0 - 0.8 * variance) / below, 1.6 * variance / below, jnp.sqrt(6.4 * variance) / below


def folded(picked, rows):
    size = picked.shape[1]
    lane = lax.broadcasted_iota(jnp.int32, (size, size // rows), 0)
    to = lax.broadcasted_iota(jnp.int32, (size, size // rows), 1)
    ones = jnp.where((lane >= to * rows) & (lane < to * rows + rows), 1.0, 0.0).astype(jnp.bfloat16)
    total = None
    for _ in range(3):
        part = picked.astype(jnp.bfloat16)
        picked = picked - part.astype(jnp.float32)
        part = jnp.dot(part, ones, preferred_element_type=jnp.float32)
        total = part if total is None else total + part
    return total


def picked_rows(product, rows, chains):
    row = lax.rem(lax.broadcasted_iota(jnp.int32, (chains, product.shape[1]), 1), rows)
    out = product[:chains]
    for x in range(1, rows):
        out = jnp.where(row == x, product[x * chains : (x + 1) * chains], out)
    return out


def across_lanes(left, right):
    return lax.dot_general(left, right, (((1,), (1,)), ((), ())), preferred_element_type=jnp.float32)


def early_kernel(basis, own, noise, fields, coefs, picked, *, rows, chains, steps):
    ranks = basis.shape[0] // steps
    width = basis.shape[2]
    spot = Packed(rows, chains)
    log = jnp.concatenate([own[: spot.split, :], own[spot.split + 2 * rows :, :]], 0)
    left = jnp.concatenate([log.astype(jnp.bfloat16), noise[...]], 0)
    for j in range(steps):
        block = basis[pl.ds(j * ranks, ranks)].reshape(ranks * rows, width)
        cut = pl.ds(j * ranks * rows, ranks * rows)
        fields[cut, :] = block
        product = across_lanes(left, block)
        half = rows * chains
        picked[:chains, cut] = picked_rows(product[:half], rows, chains)
        picked[chains:, cut] = picked_rows(product[half:], rows, chains)
    coefs[...] = folded(picked[...], rows)


def gradient_kernel(
    got, kept, state, log, fields, early, eigenvalues, sums, gradient, picked, *, rows, groups
):
    tile = total_of(got)
    chains = groups * SUB
    spot = Packed(rows, chains)
    for g in range(groups):
        weights = weights_of(tile, g)
        for r in range(rows):
            value = weights[0] * kept[0, r, g]
            for k in range(1, ITERS):
                value = value + weights[k] * kept[k, r, g]
            at = spot.log(r, g)
            value = -jnp.exp(log[at : at + SUB, :]) * value * state[r, g]
            at = r * chains + g * SUB
            gradient[at : at + SUB, :] = value
    left = gradient[...].astype(jnp.bfloat16)
    size = fields.shape[0]
    step = min(size, 2 * LANES)
    for start in range(0, size, step):
        product = across_lanes(left, fields[start : start + step, :])
        picked[:, start : start + step] = picked_rows(product, rows, chains)
    keep, drift, _ = factors(eigenvalues[...])
    state_coef, noise_coef = early[:chains], early[chains:]
    sums[:chains] = keep * state_coef - drift * folded(picked[...], rows)
    sums[chains:] = -0.6 * state_coef - 0.8 * noise_coef


def proposal_kernel(
    sums, eigenvalues, subspace, fields, log, noise, proposal, new_coef, result, sent, *, rows, chains, steps
):
    _, _, noise_factor = factors(eigenvalues[...])
    coef = sums[:chains] + noise_factor * subspace[...]
    new_coef[...] = coef
    correction = (coef + sums[chains:]).astype(jnp.bfloat16)
    size, width = fields.shape
    rank = size // rows
    row = lax.broadcasted_iota(jnp.int32, (chains * rows, chains), 0)
    to = lax.broadcasted_iota(jnp.int32, (chains * rows, chains), 1)
    tall = jnp.where((row >= to * rows) & (row < to * rows + rows), 1.0, 0.0).astype(jnp.bfloat16)
    lane = lax.broadcasted_iota(jnp.int32, (rank, size), 1)
    to = lax.broadcasted_iota(jnp.int32, (rank, size), 0)
    wide = jnp.where((lane >= to * rows) & (lane < to * rows + rows), 1.0, 0.0).astype(jnp.bfloat16)
    left = jnp.dot(tall, correction, preferred_element_type=jnp.float32).astype(jnp.bfloat16)
    left = jnp.dot(left, wide, preferred_element_type=jnp.float32)
    row = lax.rem(lax.broadcasted_iota(jnp.int32, left.shape, 0), rows)
    lane = lax.rem(lax.broadcasted_iota(jnp.int32, left.shape, 1), rows)
    left = jnp.where(row == lane, left, 0.0).astype(jnp.bfloat16)
    copies = []
    for j in range(steps):
        cut = pl.ds(j * (width // steps), width // steps)
        product = jnp.dot(left, fields[:, cut], preferred_element_type=jnp.float32)
        for c in range(chains):
            base = 0.6 * log[c, :, cut] + 0.8 * noise[c, :, cut]
            result[c, :, cut] = base + product[c * rows : (c + 1) * rows]
        copies.append(
            pltpu.make_async_copy(result.at[:, :, cut], proposal.at[:, :, cut], sent.at[j])
        )
        copies[-1].start()
    for copy in copies:
        copy.wait()


def call(kernel, outs, args, scratch=(), spaces=(), out_spaces=(), **static):
    spaces = dict(spaces)
    out_spaces = dict(out_spaces)
    sizes = [math.prod(s) * 4 if isinstance(s, tuple) else 0 for s in scratch]
    limit = sum(sizes) + static.pop("more", 0) + 3 * 1024 * 1024
    outs = [out if len(out) == 2 and not isinstance(out[0], int) else (out, jnp.float32) for out in outs]
    return pl.pallas_call(
        functools.partial(kernel, **static),
        out_shape=[jax.ShapeDtypeStruct(*out) for out in outs],
        in_specs=[pl.BlockSpec(memory_space=spaces.get(i, pltpu.VMEM)) for i in range(len(args))],
        out_specs=[pl.BlockSpec(memory_space=out_spaces.get(i, pltpu.VMEM)) for i in range(len(outs))],
        scratch_shapes=[pltpu.VMEM(s, jnp.float32) if isinstance(s, tuple) else s for s in scratch],
        compiler_params=pltpu.CompilerParams(vmem_limit_bytes=limit),
    )(*args)


def per_device(
    source,
    observed,
    precision,
    conductivity,
    log_field,
    noise_field,
    subspace_noise,
    eigenvalues,
    basis,
):
    halo = ITERS
    chains, rows, width = log_field.shape
    rank = basis.shape[0]
    groups = chains // SUB
    position = lax.axis_index(AXIS)
    devices = lax.axis_size(AXIS)

    assert rows == halo and chains % SUB == 0
    above = halo - 1
    spot = Packed(rows, chains)
    far = shifted(conductivity[:1], -2)
    place = jnp.stack([position, devices - 1 - position])
    log_rows = jnp.transpose(log_field, (1, 0, 2)).reshape(rows * chains, width)
    packed = jnp.concatenate(
        [log_rows[: spot.split], source, conductivity, log_rows[spot.split :]], 0
    )
    before = shifted(packed, 1)
    after = shifted(packed, -1)
    noise_rows = jnp.transpose(noise_field, (1, 0, 2)).astype(jnp.bfloat16)
    steps = math.gcd(8, rank)
    fields, early = call(
        early_kernel,
        [((rows * rank, width), jnp.bfloat16), (2 * chains, rank)],
        [
            basis,
            packed,
            noise_rows.reshape(rows * chains, width),
        ],
        [(2 * chains, rows * rank)],
        rows=rows,
        chains=chains,
        steps=steps,
    )
    early, precision, observed = lax.optimization_barrier((early, precision, observed))
    far_before = jnp.concatenate([before[spot.upward :], precision, observed], 0)
    far_after = jnp.concatenate([after[: spot.downward], precision, observed], 0)
    far_before = shifted(far_before, 1)
    far_after = shifted(far_after, -1)

    total = rows + above + halo
    block = (groups, SUB, width)
    tiles = (devices, SUB // 2, LANES)
    moments = [(len(SHIFTS), rows + 1) + block, (len(SHIFTS), rows) + block]
    frames = [(total - 2 * k,) + block for k in range(ITERS)]
    images = [(total - 2 * k - 2,) + block for k in range(ITERS - 1)]
    sent, *vectors, inverse, across, along = call(
        forward_kernel,
        [tiles] + frames + [(total,) + block, (total, SUB, width), (total + 1, SUB, width)],
        [early, place, packed, before, after, far],
        [(total + 2, SUB, width), (rows, SUB, width)] + moments + images,
        spaces={1: pltpu.SMEM},
        rows=rows,
        groups=groups,
    )
    sent, kept, state = call(
        adjoint_kernel,
        [tiles, (ITERS, rows) + block, (rows,) + block],
        [place, exchanged(sent), *vectors, inverse, across, along]
        + [before, after, far_before, far_after, precision, observed],
        [
            (rows,) + block,
            (ITERS, 6) + block,
            (6,) + block,
            (6, SUB, width),
            (6, SUB, width),
        ]
        + moments
        + frames
        + images,
        spaces={0: pltpu.SMEM},
        rows=rows,
        groups=groups,
    )
    (sums,) = call(
        gradient_kernel,
        [(2 * chains, rank)],
        [exchanged(sent), kept, state, packed, fields, early, eigenvalues[None]],
        [(rows * chains, width), (chains, rows * rank)],
        rows=rows,
        groups=groups,
    )
    steps = math.gcd(4, width // LANES)
    proposal, new_coef = call(
        proposal_kernel,
        [log_field.shape, (chains, rank)],
        [summed(sums), eigenvalues[None], subspace_noise, fields, log_field, noise_field],
        [log_field.shape, pltpu.SemaphoreType.DMA((steps,))],
        out_spaces={0: pl.ANY},
        rows=rows,
        chains=chains,
        steps=steps,
    )
    return (proposal, new_coef)


def solution(mesh):
    return jax.shard_map(
        per_device,
        mesh=mesh,
        in_specs=(
            P("rows", None),
            P("rows", None),
            P("rows", None),
            P("rows", None),
            P(None, "rows", None),
            P(None, "rows", None),
            P(),
            P(),
            P(None, "rows", None),
        ),
        out_specs=(P(None, "rows", None), P()),
        check_vma=False,
    )
```

profile of v0, /device:TPU:0, one launch (start us, length us, event | category | flops | bytes accessed | tf_op | source)
XLA Modules:
  0.0 90.5 jit_solution(1858647030182653549)
XLA Ops:
  0.6 0.0 copy-start.9
  0.6 0.0 copy-start.10
  0.6 0.0 copy-start.2
  0.7 1.6 %fusion = (f32[2,16,2048]{2,0,1:T(2,128)S(1)}, f32[2,16,2048]{2,0,1:T(2,128)S(1)}) fusion(f32[4,16,2048]{2,0,1:T(4,128)} %bitcast.9), kind=kLoop, calls=%fused_computation.7 | loop fusion | bytes 1048576 | tf_op jit(solution)/shard_map/slice | solution.py:566
  2.3 0.2 copy.11
  2.4 0.2 copy.12
  2.7 1.3 %collective-permute-start.1 = (f32[72,2048]{1,0:T(8,128)S(1)}, f32[72,2048]{1,0:T(8,128)S(1)}, u32[]{:S(2)}, u32[]{:S(2)}) collective-permute-start(f32[72,2048]{1,0:T(8,128)S(1)} %pad_maximum_fusion.own.log), channel_id=1, source_target_pairs={{1,0},{2,1},{3,2},{4,3},{5,4},{6,5},{7,6},{8,7},{9,8},{10,9},{11,1... | collective-permute-start | bytes 1769480 | tf_op jit(solution)/shard_map/ppermute | solution.py:21
  4.0 3.1 %collective-permute-start = (f32[72,2048]{1,0:T(8,128)S(1)}, f32[72,2048]{1,0:T(8,128)S(1)}, u32[]{:S(2)}, u32[]{:S(2)}) collective-permute-start(f32[72,2048]{1,0:T(8,128)S(1)} %pad_maximum_fusion.own.log), channel_id=1, source_target_pairs={{0,1},{1,2},{2,3},{3,4},{4,5},{5,6},{6,7},{7,8},{8,9},{9,10},{10,1... | collective-permute-start | bytes 1769480 | tf_op jit(solution)/shard_map/ppermute | solution.py:21
  7.1 1.1 %convert_bitcast_fusion = bf16[4,16,2048]{2,0,1:T(4,128)(2,1)S(1)} fusion(f32[16,4,2048]{2,1,0:T(4,128)} %noise.1), kind=kLoop, calls=%fused_computation.3 | loop fusion | flops 131072 | bytes 786432 | tf_op jit(solution)/shard_map/convert_element_type | solution.py:570
  8.2 0.2 copy.13
  8.4 0.0 copy-start.5
  8.4 0.0 copy-start.6
  8.4 1.9 %shard_map.104 = (bf16[1024,2048]{1,0:T(8,128)(2,1)S(1)}, f32[32,256]{1,0:T(8,128)S(1)}) custom-call(bf16[256,4,2048]{2,1,0:T(4,128)(2,1)S(1)} %copy-done.2, f32[72,2048]{1,0:T(8,128)S(1)} %pad_maximum_fusion.own.log, bf16[64,2048]{1,0:T(8,128)(2,1)S(1)} %bitcast.10), custom_call_target="tpu_custom_call" | custom-call | tf_op jit(solution)/shard_map/pallas_call | solution.py:531
  10.3 1.9 %copy-done = bf16[1024,2048]{1,0:T(8,128)(2,1)} copy-done((bf16[1024,2048]{1,0:T(8,128)(2,1)}, bf16[1024,2048]{1,0:T(8,128)(2,1)S(1)}, u32[]{:S(2)}) %copy-start) | copy-done | bytes 4194328
  12.3 0.0 collective-permute-done.1.after
  12.3 0.0 copy-done.5
  12.3 0.0 copy-done.6
  12.4 1.3 %collective-permute-start.4 = (f32[64,2048]{1,0:T(8,128)S(1)}, f32[64,2048]{1,0:T(8,128)S(1)}, u32[]{:S(2)}, u32[]{:S(2)}) collective-permute-start(f32[64,2048]{1,0:T(8,128)S(1)} %pad_maximum_fusion.1), channel_id=1, source_target_pairs={{1,0},{2,1},{3,2},{4,3},{5,4},{6,5},{7,6},{8,7},{9,8},{10,9},{11,1... | collective-permute-start | bytes 1572872 | tf_op jit(solution)/shard_map/ppermute | solution.py:21
  13.7 0.0 collective-permute-done.before
  13.7 0.8 pad_maximum_fusion.2
  14.5 10.9 %collective-permute-start.3 = (f32[48,2048]{1,0:T(8,128)}, f32[48,2048]{1,0:T(8,128)S(1)}, u32[]{:S(2)}, u32[]{:S(2)}) collective-permute-start(f32[48,2048]{1,0:T(8,128)} %pad_maximum_fusion.2), channel_id=1, source_target_pairs={{0,1},{1,2},{2,3},{3,4},{4,5},{5,6},{6,7},{7,8},{8,9},{9,10},{10,1... | collective-permute-start | bytes 1179656 | tf_op jit(solution)/shard_map/ppermute | solution.py:21
  25.4 1.3 %collective-permute-start.2 = (f32[1,2048]{1,0:T(1,128)S(1)}, f32[1,2048]{1,0:T(1,128)S(1)}, u32[]{:S(2)}, u32[]{:S(2)}) collective-permute-start(f32[1,2048]{1,0:T(1,128)S(1)} %slice.25), channel_id=1, source_target_pairs={{2,0},{3,1},{4,2},{5,3},{6,4},{7,5},{8,6},{9,7},{10,8},{11,9},{12,... | collective-permute-start | bytes 24584 | tf_op jit(solution)/shard_map/ppermute | solution.py:21
  26.7 0.1 pad_add_fusion.place
  26.8 4.6 %collective-permute-done.2.far = f32[1,2048]{1,0:T(1,128)S(1)} collective-permute-done((f32[1,2048]{1,0:T(1,128)S(1)}, f32[1,2048]{1,0:T(1,128)S(1)}, u32[]{:S(2)}, u32[]{:S(2)}) %collective-permute-start.2) | collective-permute-done | bytes 8224 | tf_op jit(solution)/shard_map/ppermute | solution.py:21
  31.4 5.7 %shard_map.105 = (f32[32,4,128]{2,1,0:T(4,128)S(1)}, f32[11,2,8,2048]{3,2,1,0:T(8,128)S(1)}, f32[9,2,8,2048]{3,2,1,0:T(8,128)S(1)}, f32[7,2,8,2048]{3,2,1,0:T(8,...) custom-call(f32[32,256]{1,0:T(8,128)S(1)} %get-tuple-element.19._.ea, ...), custom_call_target="tpu_custom_call" | custom-call | tf_op jit(solution)/shard_map/pallas_call | solution.py:531
  37.1 17.7 %all_to_all.10.got = f32[32,4,128]{2,1,0:T(4,128)S(1)} all-to-all(f32[32,4,128]{2,1,0:T(4,128)S(1)} %get-tuple-element.20), channel_id=1, replica_groups=mesh['rows'=32] {'rows'}, dimensions={0} | all-to-all | bytes 131072 | tf_op jit(solution)/shard_map/all_to_all | solution.py:25
  54.8 0.0 collective-permute-done.3.far_before
  54.8 0.0 collective-permute-done.4.far_after
  54.8 0.0 copy-start.8
  54.8 8.0 %shard_map.106 = (f32[32,4,128]{2,1,0:T(4,128)S(1)}, f32[4,4,2,8,2048]{4,3,2,1,0:T(8,128)S(1)}, f32[4,2,8,2048]{3,2,1,0:T(8,128)S(1)}) custom-call(s32[2]{0:T(128)S(1)} %pad_add_fusion.place, f32[32,4,128]{2,1,0:T(4,128)S(1)} %all_to_all.10.got, f32[11,2,8,2048]{3,2,1,0:T(8,128)S(1)} %get-tuple-element.21.f0, f32[9,2,8,2048]{3,2,1,0:T(8,128)S(1)} %get-tuple-element.22.f1, ...), custom_call_target="tpu_custom_call" | custom-call | tf_op jit(solution)/shard_map/pallas_call | solution.py:531
  62.8 9.1 %all_to_all.11.got = f32[32,4,128]{2,1,0:T(4,128)S(1)} all-to-all(f32[32,4,128]{2,1,0:T(4,128)S(1)} %get-tuple-element.30), channel_id=1, replica_groups=mesh['rows'=32] {'rows'}, dimensions={0} | all-to-all | bytes 131072 | tf_op jit(solution)/shard_map/all_to_all | solution.py:25
  71.9 0.0 copy-start.7
  71.9 2.3 %shard_map.107 = f32[32,256]{1,0:T(8,128)S(1)} custom-call(f32[32,4,128]{2,1,0:T(4,128)S(1)} %all_to_all.11.got, f32[4,4,2,8,2048]{4,3,2,1,0:T(8,128)S(1)} %get-tuple-element.31.kept, f32[4,2,8,2048]{3,2,1,0:T(8,128)S(1)} %get-tuple-element.32.state, f32[72,2048]{1,0:T(8,128)S(1)} %pad_maximum_fusion.own.log, bf16[1024,2048]{1,0:T(8,128)(2,1)S(1)} %copy-done.1, ...), custom_call_target="tpu_custom_call" | custom-call | tf_op jit(solution)/shard_map/pallas_call | solution.py:531
  74.2 0.1 collective-permute-start.5
  74.3 1.1 %collective-permute-done.5 = f32[32,256]{1,0:T(8,128)S(1)} collective-permute-done((f32[32,256]{1,0:T(8,128)S(1)}, f32[32,256]{1,0:T(8,128)S(1)}, u32[]{:S(2)}, u32[]{:S(2)}) %collective-permute-start.5) | collective-permute-done | bytes 32800 | tf_op jit(solution)/shard_map/ppermute | solution.py:37
  75.4 0.7 collective-permute-start.8
  76.2 1.2 %collective-permute-start.7 = (f32[32,256]{1,0:T(8,128)S(1)}, f32[32,256]{1,0:T(8,128)S(1)}, u32[]{:S(2)}, u32[]{:S(2)}) collective-permute-start(f32[32,256]{1,0:T(8,128)S(1)} %add.21), channel_id=1, source_target_pairs={{0,4},{1,5},{2,6},{3,7},{4,0},{5,1},{6,2},{7,3},{8,12},{9,13},{10,... | collective-permute-start | bytes 98312 | tf_op jit(solution)/shard_map/ppermute | solution.py:37
  77.3 1.6 %collective-permute-start.6 = (f32[32,256]{1,0:T(8,128)S(1)}, f32[32,256]{1,0:T(8,128)S(1)}, u32[]{:S(2)}, u32[]{:S(2)}) collective-permute-start(f32[32,256]{1,0:T(8,128)S(1)} %add.21), channel_id=1, source_target_pairs={{0,2},{1,3},{2,0},{3,1},{4,6},{5,7},{6,4},{7,5},{8,10},{9,11},{10,... | collective-permute-start | bytes 98312 | tf_op jit(solution)/shard_map/ppermute | solution.py:37
  78.9 1.6 %collective-permute-done.8 = f32[32,256]{1,0:T(8,128)S(1)} collective-permute-done((f32[32,256]{1,0:T(8,128)S(1)}, f32[32,256]{1,0:T(8,128)S(1)}, u32[]{:S(2)}, u32[]{:S(2)}) %collective-permute-start.8) | collective-permute-done | bytes 32800 | tf_op jit(solution)/shard_map/ppermute | solution.py:37
  80.5 0.0 collective-permute-done.7
  80.5 0.7 collective-permute-done.6
  81.3 0.9 %collective-permute-start.11 = (f32[32,256]{1,0:T(8,128)S(1)}, f32[32,256]{1,0:T(8,128)S(1)}, u32[]{:S(2)}, u32[]{:S(2)}) collective-permute-start(f32[32,256]{1,0:T(8,128)S(1)} %add_add_fusion.1), channel_id=1, source_target_pairs={{0,24},{1,25},{2,26},{3,27},{4,28},{5,29},{6,30},{7,31},{8,16},{9,... | collective-permute-start | bytes 98312 | tf_op jit(solution)/shard_map/ppermute | solution.py:37
  82.2 1.2 %collective-permute-start.10 = (f32[32,256]{1,0:T(8,128)S(1)}, f32[32,256]{1,0:T(8,128)S(1)}, u32[]{:S(2)}, u32[]{:S(2)}) collective-permute-start(f32[32,256]{1,0:T(8,128)S(1)} %add_add_fusion.1), channel_id=1, source_target_pairs={{0,16},{1,17},{2,18},{3,19},{4,20},{5,21},{6,22},{7,23},{8,24},{9,... | collective-permute-start | bytes 98312 | tf_op jit(solution)/shard_map/ppermute | solution.py:37
  83.4 2.3 %collective-permute-start.9 = (f32[32,256]{1,0:T(8,128)S(1)}, f32[32,256]{1,0:T(8,128)S(1)}, u32[]{:S(2)}, u32[]{:S(2)}) collective-permute-start(f32[32,256]{1,0:T(8,128)S(1)} %add_add_fusion.1), channel_id=1, source_target_pairs={{0,8},{1,9},{2,10},{3,11},{4,12},{5,13},{6,14},{7,15},{8,0},{9,1},... | collective-permute-start | bytes 98312 | tf_op jit(solution)/shard_map/ppermute | solution.py:37
  85.7 1.4 %collective-permute-done.11 = f32[32,256]{1,0:T(8,128)S(1)} collective-permute-done((f32[32,256]{1,0:T(8,128)S(1)}, f32[32,256]{1,0:T(8,128)S(1)}, u32[]{:S(2)}, u32[]{:S(2)}) %collective-permute-start.11) | collective-permute-done | bytes 32800 | tf_op jit(solution)/shard_map/ppermute | solution.py:37
  87.1 0.7 collective-permute-done.10
  87.8 0.0 collective-permute-done.9
  87.9 2.5 %shard_map.108 = (f32[16,4,2048]{2,1,0:T(4,128)}, f32[16,256]{1,0:T(8,128)}) custom-call(f32[32,256]{1,0:T(8,128)S(1)} %add_add_fusion.sums, f32[1,256]{1,0:T(1,128)S(1)} %bitcast.12, f32[16,256]{1,0:T(8,128)S(1)} %copy-done.7, bf16[1024,2048]{1,0:T(8,128)(2,1)S(1)} %copy-done.1, f32[16,4,2048]{2,1,0:T(4,128)S(1)} %copy-done.3, f32[16,4,2048]{2,1,0:T(4,128)S(1)} %copy-done.4), custom_call_target="tpu_custom_call" | custom-call | tf_op jit(solution)/shard_map/pallas_call | solution.py:531
  (20 shorter events, 0.2 us)
Async XLA Ops:
  0.6 2.0 %copy-start.9 = (f32[4,2048]{1,0:T(4,128)S(1)}, f32[4,2048]{1,0:T(4,128)}, u32[]{:S(2)}) copy-start(f32[4,2048]{1,0:T(4,128)} %param.12) | copy-start | bytes 98308
  0.6 2.0 %copy-start.10 = (f32[4,2048]{1,0:T(4,128)S(1)}, f32[4,2048]{1,0:T(4,128)}, u32[]{:S(2)}) copy-start(f32[4,2048]{1,0:T(4,128)} %param.9) | copy-start | bytes 98308
  0.6 7.7 %copy-start.2 = (bf16[256,4,2048]{2,1,0:T(4,128)(2,1)S(1)}, bf16[256,4,2048]{2,1,0:T(4,128)(2,1)}, u32[]{:S(2)}) copy-start(bf16[256,4,2048]{2,1,0:T(4,128)(2,1)} %basis.1) | copy-start | bytes 12582916
  2.7 9.6 %collective-permute-start.1 = (f32[72,2048]{1,0:T(8,128)S(1)}, f32[72,2048]{1,0:T(8,128)S(1)}, u32[]{:S(2)}, u32[]{:S(2)}) collective-permute-start(f32[72,2048]{1,0:T(8,128)S(1)} %pad_maximum_fusion.own.log), channel_id=1, source_target_pairs={{1,0},{2,1},{3,2},{4,3},{5,4},{6,5},{7,6},{8,7},{9,8},{10,9},{11,1... | collective-permute-start | bytes 1769480 | tf_op jit(solution)/shard_map/ppermute | solution.py:21
  4.0 9.7 %collective-permute-start = (f32[72,2048]{1,0:T(8,128)S(1)}, f32[72,2048]{1,0:T(8,128)S(1)}, u32[]{:S(2)}, u32[]{:S(2)}) collective-permute-start(f32[72,2048]{1,0:T(8,128)S(1)} %pad_maximum_fusion.own.log), channel_id=1, source_target_pairs={{0,1},{1,2},{2,3},{3,4},{4,5},{5,6},{6,7},{7,8},{8,9},{9,10},{10,1... | collective-permute-start | bytes 1769480 | tf_op jit(solution)/shard_map/ppermute | solution.py:21
  8.4 3.9 %copy-start.5 = (f32[4,2048]{1,0:T(4,128)S(1)}, f32[4,2048]{1,0:T(4,128)}, u32[]{:S(2)}) copy-start(f32[4,2048]{1,0:T(4,128)} %observed) | copy-start | bytes 98308
  8.4 3.9 %copy-start.6 = (f32[4,2048]{1,0:T(4,128)S(1)}, f32[4,2048]{1,0:T(4,128)}, u32[]{:S(2)}) copy-start(f32[4,2048]{1,0:T(4,128)} %precision) | copy-start | bytes 98308
  10.3 2.0 %copy-start = (bf16[1024,2048]{1,0:T(8,128)(2,1)}, bf16[1024,2048]{1,0:T(8,128)(2,1)S(1)}, u32[]{:S(2)}) copy-start(bf16[1024,2048]{1,0:T(8,128)(2,1)S(1)} %get-tuple-element.33.fields) | copy-start | bytes 12582916
  12.4 42.5 %collective-permute-start.4 = (f32[64,2048]{1,0:T(8,128)S(1)}, f32[64,2048]{1,0:T(8,128)S(1)}, u32[]{:S(2)}, u32[]{:S(2)}) collective-permute-start(f32[64,2048]{1,0:T(8,128)S(1)} %pad_maximum_fusion.1), channel_id=1, source_target_pairs={{1,0},{2,1},{3,2},{4,3},{5,4},{6,5},{7,6},{8,7},{9,8},{10,9},{11,1... | collective-permute-start | bytes 1572872 | tf_op jit(solution)/shard_map/ppermute | solution.py:21
  14.5 40.3 %collective-permute-start.3 = (f32[48,2048]{1,0:T(8,128)}, f32[48,2048]{1,0:T(8,128)S(1)}, u32[]{:S(2)}, u32[]{:S(2)}) collective-permute-start(f32[48,2048]{1,0:T(8,128)} %pad_maximum_fusion.2), channel_id=1, source_target_pairs={{0,1},{1,2},{2,3},{3,4},{4,5},{5,6},{6,7},{7,8},{8,9},{9,10},{10,1... | collective-permute-start | bytes 1179656 | tf_op jit(solution)/shard_map/ppermute | solution.py:21
  25.4 6.0 %collective-permute-start.2 = (f32[1,2048]{1,0:T(1,128)S(1)}, f32[1,2048]{1,0:T(1,128)S(1)}, u32[]{:S(2)}, u32[]{:S(2)}) collective-permute-start(f32[1,2048]{1,0:T(1,128)S(1)} %slice.25), channel_id=1, source_target_pairs={{2,0},{3,1},{4,2},{5,3},{6,4},{7,5},{8,6},{9,7},{10,8},{11,9},{12,... | collective-permute-start | bytes 24584 | tf_op jit(solution)/shard_map/ppermute | solution.py:21
  54.8 17.1 %copy-start.1 = (bf16[1024,2048]{1,0:T(8,128)(2,1)S(1)}, bf16[1024,2048]{1,0:T(8,128)(2,1)}, u32[]{:S(2)}) copy-start(bf16[1024,2048]{1,0:T(8,128)(2,1)} %copy-done) | copy-start | bytes 12582916
  54.8 17.1 %copy-start.8 = (f32[256]{0:T(256)S(1)}, f32[256]{0:T(256)}, u32[]{:S(2)}) copy-start(f32[256]{0:T(256)} %param.16) | copy-start | bytes 3076
  71.9 15.9 %copy-start.3 = (f32[16,4,2048]{2,1,0:T(4,128)S(1)}, f32[16,4,2048]{2,1,0:T(4,128)}, u32[]{:S(2)}) copy-start(f32[16,4,2048]{2,1,0:T(4,128)} %log.1) | copy-start | bytes 1572868
  71.9 15.9 %copy-start.4 = (f32[16,4,2048]{2,1,0:T(4,128)S(1)}, f32[16,4,2048]{2,1,0:T(4,128)}, u32[]{:S(2)}) copy-start(f32[16,4,2048]{2,1,0:T(4,128)} %noise.1) | copy-start | bytes 1572868
  71.9 15.9 %copy-start.7 = (f32[16,256]{1,0:T(8,128)S(1)}, f32[16,256]{1,0:T(8,128)}, u32[]{:S(2)}) copy-start(f32[16,256]{1,0:T(8,128)} %subspace.1) | copy-start | bytes 49156
  74.2 1.2 %collective-permute-start.5 = (f32[32,256]{1,0:T(8,128)S(1)}, f32[32,256]{1,0:T(8,128)S(1)}, u32[]{:S(2)}, u32[]{:S(2)}) collective-permute-start(f32[32,256]{1,0:T(8,128)S(1)} %shard_map.107), channel_id=1, source_target_pairs={{0,1},{1,0},{2,3},{3,2},{4,5},{5,4},{6,7},{7,6},{8,9},{9,8},{10,11... | collective-permute-start | bytes 98312 | tf_op jit(solution)/shard_map/ppermute | solution.py:37
  75.4 5.1 %collective-permute-start.8 = (f32[32,256]{1,0:T(8,128)S(1)}, f32[32,256]{1,0:T(8,128)S(1)}, u32[]{:S(2)}, u32[]{:S(2)}) collective-permute-start(f32[32,256]{1,0:T(8,128)S(1)} %add.21), channel_id=1, source_target_pairs={{0,6},{1,7},{2,4},{3,5},{4,2},{5,3},{6,0},{7,1},{8,14},{9,15},{10,... | collective-permute-start | bytes 98312 | tf_op jit(solution)/shard_map/ppermute | solution.py:37
  76.2 4.4 %collective-permute-start.7 = (f32[32,256]{1,0:T(8,128)S(1)}, f32[32,256]{1,0:T(8,128)S(1)}, u32[]{:S(2)}, u32[]{:S(2)}) collective-permute-start(f32[32,256]{1,0:T(8,128)S(1)} %add.21), channel_id=1, source_target_pairs={{0,4},{1,5},{2,6},{3,7},{4,0},{5,1},{6,2},{7,3},{8,12},{9,13},{10,... | collective-permute-start | bytes 98312 | tf_op jit(solution)/shard_map/ppermute | solution.py:37
  77.3 3.9 %collective-permute-start.6 = (f32[32,256]{1,0:T(8,128)S(1)}, f32[32,256]{1,0:T(8,128)S(1)}, u32[]{:S(2)}, u32[]{:S(2)}) collective-permute-start(f32[32,256]{1,0:T(8,128)S(1)} %add.21), channel_id=1, source_target_pairs={{0,2},{1,3},{2,0},{3,1},{4,6},{5,7},{6,4},{7,5},{8,10},{9,11},{10,... | collective-permute-start | bytes 98312 | tf_op jit(solution)/shard_map/ppermute | solution.py:37
  81.3 5.9 %collective-permute-start.11 = (f32[32,256]{1,0:T(8,128)S(1)}, f32[32,256]{1,0:T(8,128)S(1)}, u32[]{:S(2)}, u32[]{:S(2)}) collective-permute-start(f32[32,256]{1,0:T(8,128)S(1)} %add_add_fusion.1), channel_id=1, source_target_pairs={{0,24},{1,25},{2,26},{3,27},{4,28},{5,29},{6,30},{7,31},{8,16},{9,... | collective-permute-start | bytes 98312 | tf_op jit(solution)/shard_map/ppermute | solution.py:37
  82.2 5.6 %collective-permute-start.10 = (f32[32,256]{1,0:T(8,128)S(1)}, f32[32,256]{1,0:T(8,128)S(1)}, u32[]{:S(2)}, u32[]{:S(2)}) collective-permute-start(f32[32,256]{1,0:T(8,128)S(1)} %add_add_fusion.1), channel_id=1, source_target_pairs={{0,16},{1,17},{2,18},{3,19},{4,20},{5,21},{6,22},{7,23},{8,24},{9,... | collective-permute-start | bytes 98312 | tf_op jit(solution)/shard_map/ppermute | solution.py:37
  83.4 4.4 %collective-permute-start.9 = (f32[32,256]{1,0:T(8,128)S(1)}, f32[32,256]{1,0:T(8,128)S(1)}, u32[]{:S(2)}, u32[]{:S(2)}) collective-permute-start(f32[32,256]{1,0:T(8,128)S(1)} %add_add_fusion.1), channel_id=1, source_target_pairs={{0,8},{1,9},{2,10},{3,11},{4,12},{5,13},{6,14},{7,15},{8,0},{9,1},... | collective-permute-start | bytes 98312 | tf_op jit(solution)/shard_map/ppermute | solution.py:37
where the time goes:
time: 90.8 us; the launch traced here: 90.5 us
  blocking collectives  26.8 us (30%)
  starting transfers between devices  25.9 us (29%)
  Pallas kernels  20.3 us (22%)
  waiting for transfers between devices  10.1 us (11%)
  local copies, waits for them, and re-layouts  4.14 us (5%)
  other arithmetic  2.11 us (2%)
  between operations  1.08 us (1%)
    all_to_all x2, blocking collectives, exchanged(): return lax.all_to_all(value, AXIS, 0, 0)  26.8 us
    pallas_call x5, Pallas kernels, call(): pl.pallas_call(functools.partial(kernel, **static), out_shape=[jax.ShapeD...  20.3 us
    ppermute x5, starting transfers between devices, shifted(): return lax.ppermute(value, AXIS, pairs)  17.9 us
    ppermute x7, starting transfers between devices, summed(): lax.ppermute(value, AXIS, [(i, i ^ k * stride) for i in range(count)])  8.06 us
    ppermute x7, waiting for transfers between devices, summed(): lax.ppermute(value, AXIS, [(i, i ^ k * stride) for i in range(count)])  5.5 us
    ppermute x5, waiting for transfers between devices, shifted(): return lax.ppermute(value, AXIS, pairs)  4.6 us
    unnamed x22, local copies, waits for them, and re-layouts  1.99 us
  transfers between devices with their start and end apart: 12, of which 6 were waited for; matrix products, arithmetic and copies ran while one was open for 2% of the time, Pallas kernels for 8%

commit v1 on v0

--- a/solution.py
+++ b/solution.py
@@ -9,7 +9,7 @@
 from jax.sharding import PartitionSpec as P
 
 ITERS = 4
-SHIFTS = (0.0, 0.5, 1.0)
+SHIFTS = (0.0, 0.75)
 AXIS = "rows"
 SUB, LANES = 8, 128
 SUMS = 2 * ITERS * len(SHIFTS)
@@ -99,6 +99,13 @@
     return chosen
 
 
+def folds_of(groups):
+    folds = SUB
+    while folds * groups * SUMS > LANES:
+        folds //= 2
+    return folds
+
+
 def krylov(vectors, images, inverse, across, along):
     width = across.shape[-1]
     groups = inverse.shape[1]
@@ -120,12 +127,14 @@
     above = ITERS - 1
     for index, shift in enumerate(SHIFTS):
         for g in range(groups):
-            for r in range(rows + 1):
-                v = [vectors[k][r + above - k, g] for k in range(ITERS)]
-                thirds[index, r, g] = differences(v, shift)[ITERS - 1]
+            if shift != 0.0:
+                for r in range(rows + 1):
+                    v = [vectors[k][r + above - k, g] for k in range(ITERS)]
+                    thirds[r, g] = differences(v, shift)[ITERS - 1]
+            third = thirds if shift != 0.0 else vectors[ITERS - 1]
             for r in range(rows):
-                u = pltpu.roll(thirds[index, r, g], width - 1, 1)
-                u = across[above + r] * u + along[above + r + 1] * thirds[index, r + 1, g]
+                u = pltpu.roll(third[r, g], width - 1, 1)
+                u = across[above + r] * u + along[above + r + 1] * third[r + 1, g]
                 halves[index, r, g] = u
     lane = lax.broadcasted_iota(jnp.int32, (SUB, LANES), 1)
     tile = jnp.zeros((SUB, LANES), jnp.float32)
@@ -140,7 +149,7 @@
                 s += [images[k][r + above - k - 1, g, :, cut] for k in range(ITERS - 1)]
                 for index, shift in enumerate(SHIFTS):
                     u, t = differences(v, shift), differences(s, shift)
-                    u.append(thirds[index, r, g, :, cut])
+                    u.append((thirds if shift != 0.0 else vectors[ITERS - 1])[r, g, :, cut])
                     t.append(halves[index, r, g, :, cut])
                     for m in range(2 * ITERS):
                         slot = index * 2 * ITERS + m
@@ -154,7 +163,12 @@
             totals[last] = 2.0 * totals[last] - shift * totals[last - 1]
         for m, total in enumerate(totals):
             tile = jnp.where(lane == g * SUMS + m, jnp.sum(total, 1, keepdims=True), tile)
-    return (tile + pltpu.roll(pltpu.roll(tile, LANES // 2, 1), SUB // 2, 0))[: SUB // 2]
+    folds = folds_of(groups)
+    out = tile
+    for q in range(1, folds):
+        part = pltpu.roll(tile, q * (LANES // folds), 1)
+        out = out + pltpu.roll(part, SUB - q * (SUB // folds), 0)
+    return out[: SUB // folds]
 
 
 def spread(ref, at):
@@ -214,11 +228,12 @@
     halo = ITERS
     above = halo - 1
     total = rows + above + halo
-    spot = Packed(rows, groups * SUB)
+    chains = groups * SUB
+    spot = Packed(rows, chains)
     vectors = (v0, v1, v2, v3)
     first, last = place[0], place[1]
     for i in range(halo):
-        at = spot.cond(rows - halo + i)
+        at = spot.cond(rows - halo + i) - chains
         cond[i] = jnp.where(first == 0, spread(own, spot.cond(0)), spread(before, at))
         at = spot.cond(i)
         cond[halo + rows + i] = jnp.where(
@@ -238,11 +253,12 @@
             ref, row, outside = own, i - above, None
         else:
             ref, row, outside = after, i - above - rows, last == 0
-        source = spread(ref, spot.source(row))
+        skipped = chains if ref is before else 0
+        source = spread(ref, spot.source(row) - skipped)
         if ref is own:
             side[row] = source
         for g in range(groups):
-            start = spot.log(row, g)
+            start = spot.log(row, g) - skipped
             value = 1.0 / (edges + jnp.exp(ref[start : start + SUB, :]))
             if outside is not None:
                 value = jnp.where(outside, 0.0, value)
@@ -259,7 +275,9 @@
     parts = [got[d] for d in range(got.shape[0])]
     while len(parts) > 1:
         parts = [a + b for a, b in zip(parts[::2], parts[1::2])] + parts[len(parts) & ~1 :]
-    return jnp.concatenate([parts[0], pltpu.roll(parts[0], LANES // 2, 1)], 0)
+    tile, folds = parts[0], SUB // parts[0].shape[0]
+    tiles = [tile] + [pltpu.roll(tile, LANES - q * (LANES // folds), 1) for q in range(1, folds)]
+    return jnp.concatenate(tiles, 0)
 
 
 def weights_of(tile, g):
@@ -314,9 +332,11 @@
         if row < -rows:
             at = row + 2 * rows
             value = spread(far_before, rows + at)
-            return jnp.where(first == 1, spread(before, spot.cond(0)), value) if at == rows - 1 else value
+            if at == rows - 1:
+                value = jnp.where(first == 1, spread(before, spot.cond(0) - chains), value)
+            return value
         if row < 0:
-            return spread(before, spot.cond(row + rows))
+            return spread(before, spot.cond(row + rows) - chains)
         if row < 2 * rows:
             return spread(after, spot.cond(row - rows))
         return spread(far_after, spot.cond(row - 2 * rows))
@@ -349,9 +369,9 @@
                 start = 2 * rows + (at - rows + 2) * chains + g * SUB
                 log = far_before[start : start + SUB, :]
             elif row < 0:
-                outside, source = first == 0, spread(before, spot.source(row + rows))
-                start = spot.log(row + rows, g)
-                log = before[start : start + SUB, :]
+                outside, source = first == 0, spread(before, spot.source(row + rows) - chains)
+                start = 2 * rows + 2 * chains + g * SUB
+                log = far_before[start : start + SUB, :]
             else:
                 at = row - 2 * rows
                 outside, source = last <= 1, spread(far_after, spot.source(at))
@@ -565,7 +585,7 @@
     packed = jnp.concatenate(
         [log_rows[: spot.split], source, conductivity, log_rows[spot.split :]], 0
     )
-    before = shifted(packed, 1)
+    before = shifted(packed[chains:], 1)
     after = shifted(packed, -1)
     noise_rows = jnp.transpose(noise_field, (1, 0, 2)).astype(jnp.bfloat16)
     steps = math.gcd(8, rank)
@@ -583,15 +603,16 @@
         steps=steps,
     )
     early, precision, observed = lax.optimization_barrier((early, precision, observed))
-    far_before = jnp.concatenate([before[spot.upward :], precision, observed], 0)
+    far_before = [before[spot.upward - chains :], packed[:chains], precision, observed]
+    far_before = jnp.concatenate(far_before, 0)
     far_after = jnp.concatenate([after[: spot.downward], precision, observed], 0)
     far_before = shifted(far_before, 1)
     far_after = shifted(far_after, -1)
 
     total = rows + above + halo
     block = (groups, SUB, width)
-    tiles = (devices, SUB // 2, LANES)
-    moments = [(len(SHIFTS), rows + 1) + block, (len(SHIFTS), rows) + block]
+    tiles = (devices, SUB // folds_of(groups), LANES)
+    moments = [(rows + 1,) + block, (len(SHIFTS), rows) + block]
     frames = [(total - 2 * k,) + block for k in range(ITERS)]
     images = [(total - 2 * k - 2,) + block for k in range(ITERS - 1)]
     sent, *vectors, inverse, across, along = call(

time: 90.8 us -> 89.9 us (0.990)
  waiting for transfers between devices: 10.1 us -> 15.5 us
  blocking collectives: 26.8 us -> 21.6 us
  starting transfers between devices: 25.9 us -> 27.7 us
  Pallas kernels: 20.3 us -> 18.7 us
    ppermute x5, waiting for transfers between devices: 4.6 us -> 10.1 us  [shifted(): return lax.ppermute(value, AXIS, pairs)]
    all_to_all x2, blocking collectives: 26.8 us -> 21.6 us  [exchanged(): return lax.all_to_all(value, AXIS, 0, 0)]
    ppermute x5, starting transfers between devices: 17.9 us -> 19.7 us  [shifted(): return lax.ppermute(value, AXIS, pairs)]
    slice x2 -> x1, local copies, waits for them, and re-layouts: 1.77 us -> 0.04 us  [per_device(): log_rows[:spot.split]]
    pallas_call x5, Pallas kernels: 20.3 us -> 18.7 us  [call(): pl.pallas_call(functools.partial(kernel, **static), out_shape=[jax.ShapeD...]
    unnamed x22 -> x23, local copies, waits for them, and re-layouts: 1.99 us -> 3.42 us
    convert_element_type x1, other arithmetic: 1.15 us -> 0.11 us  [per_device(): noise_rows = jnp.transpose(noise_field, (1, 0, 2)).astype(jnp.bfloat16)]
    concatenate x1, other arithmetic: 0.04 us -> 1.07 us  [per_device(): far_after = jnp.concatenate([after[:spot.downward], precision, observed], 0)]
  transfers between devices with their start and end apart: 12 -> 12, of which waited for: 6 -> 6; matrix products, arithmetic and copies ran while one was open for 2% -> 0% of each run, Pallas kernels for 8% -> 8%
where the time goes in v1:
time: 89.9 us; the launch traced here: 89.7 us
  starting transfers between devices  27.7 us (31%)
  blocking collectives  21.6 us (24%)
  Pallas kernels  18.7 us (21%)
  waiting for transfers between devices  15.5 us (17%)
  local copies, waits for them, and re-layouts  3.71 us (4%)
  other arithmetic  1.33 us (1%)
  between operations  1.08 us (1%)
    all_to_all x2, blocking collectives, exchanged(): return lax.all_to_all(value, AXIS, 0, 0)  21.6 us
    ppermute x5, starting transfers between devices, shifted(): return lax.ppermute(value, AXIS, pairs)  19.7 us
    pallas_call x5, Pallas kernels, call(): pl.pallas_call(functools.partial(kernel, **static), out_shape=[jax.ShapeD...  18.7 us
    ppermute x5, waiting for transfers between devices, shifted(): return lax.ppermute(value, AXIS, pairs)  10.1 us
    ppermute x7, starting transfers between devices, summed(): lax.ppermute(value, AXIS, [(i, i ^ k * stride) for i in range(count)])  8.06 us
    ppermute x7, waiting for transfers between devices, summed(): lax.ppermute(value, AXIS, [(i, i ^ k * stride) for i in range(count)])  5.37 us
    unnamed x23, local copies, waits for them, and re-layouts  3.42 us
  transfers between devices with their start and end apart: 12, of which 6 were waited for; matrix products, arithmetic and copies ran while one was open for 0% of the time, Pallas kernels for 8%

profile of v1, /device:TPU:0, one launch (start us, length us, event | category | flops | bytes accessed | tf_op | source)
XLA Modules:
  0.0 89.7 jit_solution(4691770596463203009)
XLA Ops:
  0.6 0.0 copy-start.9
  0.7 1.4 %copy.14 = f32[16,4,2048]{2,0,1:T(8,128)S(1)} copy(f32[16,4,2048]{2,1,0:T(4,128)} %log.1) | data formatting | bytes 1048576 | tf_op args[4]
  2.1 0.0 copy-start.2
  2.1 0.0 copy-done.9
  2.1 0.0 copy-done.10
  2.2 1.6 %collective-permute-start.1 = (f32[72,2048]{1,0:T(8,128)S(1)}, f32[72,2048]{1,0:T(8,128)S(1)}, u32[]{:S(2)}, u32[]{:S(2)}) collective-permute-start(f32[72,2048]{1,0:T(8,128)S(1)} %pad_maximum_fusion.4.own.log), channel_id=1, source_target_pairs={{1,0},{2,1},{3,2},{4,3},{5,4},{6,5},{7,6},{8,7},{9,8},{10,9},{11,1... | collective-permute-start | bytes 1769480 | tf_op jit(solution)/shard_map/ppermute | solution.py:21
  3.8 3.1 %collective-permute-start = (f32[56,2048]{1,0:T(8,128)S(1)}, f32[56,2048]{1,0:T(8,128)S(1)}, u32[]{:S(2)}, u32[]{:S(2)}) collective-permute-start(f32[56,2048]{1,0:T(8,128)S(1)} %slice.43), channel_id=1, source_target_pairs={{0,1},{1,2},{2,3},{3,4},{4,5},{5,6},{6,7},{7,8},{8,9},{9,10},{10,1... | collective-permute-start | bytes 1376264 | tf_op jit(solution)/shard_map/ppermute | solution.py:21
  6.9 0.1 convert_bitcast_fusion
  7.0 0.2 copy.12
  7.2 0.0 copy-done.2
  7.2 0.0 copy-start.5
  7.2 0.0 copy-start.6
  7.2 2.0 %shard_map.104 = (bf16[1024,2048]{1,0:T(8,128)(2,1)S(1)}, f32[32,256]{1,0:T(8,128)S(1)}) custom-call(bf16[256,4,2048]{2,1,0:T(4,128)(2,1)S(1)} %copy-done.2, f32[72,2048]{1,0:T(8,128)S(1)} %pad_maximum_fusion.4.own.log, bf16[64,2048]{1,0:T(8,128)(2,1)S(1)} %bitcast.13), custom_call_target="tpu_custom_call" | custom-call | tf_op jit(solution)/shard_map/pallas_call | solution.py:551
  9.2 2.0 %copy-done = bf16[1024,2048]{1,0:T(8,128)(2,1)} copy-done((bf16[1024,2048]{1,0:T(8,128)(2,1)}, bf16[1024,2048]{1,0:T(8,128)(2,1)S(1)}, u32[]{:S(2)}) %copy-start) | copy-done | bytes 4194328
  11.1 0.0 collective-permute-done.before
  11.2 0.0 collective-permute-done.1.after
  11.2 1.1 %pad_maximum_fusion = (f32[64,2048]{1,0:T(8,128)}, f32[64,2048]{1,0:T(8,128)}) fusion(f32[4,2048]{1,0:T(4,128)S(1)} %copy-done.5, f32[4,2048]{1,0:T(4,128)S(1)} %copy-done.6, f32[56,2048]{1,0:T(8,128)S(1)} %slice.46, f32[16,2048]{1,0:T(8,128)S(1)} %slice_bitcast_fusion, f32[40,2048]{1,0:T(8,128)S(1)} %slice.44), kind=kLoop, calls=%fused_computation | loop fusion | flops 655360 | bytes 2031616 | tf_op jit(solution)/shard_map/concatenate | solution.py:608
  12.3 1.3 %collective-permute-start.4 = (f32[64,2048]{1,0:T(8,128)}, f32[64,2048]{1,0:T(8,128)S(1)}, u32[]{:S(2)}, u32[]{:S(2)}) collective-permute-start(f32[64,2048]{1,0:T(8,128)} %get-tuple-element.36), channel_id=1, source_target_pairs={{1,0},{2,1},{3,2},{4,3},{5,4},{6,5},{7,6},{8,7},{9,8},{10,9},{11,1... | collective-permute-start | bytes 1572872 | tf_op jit(solution)/shard_map/ppermute | solution.py:21
  13.6 12.5 %collective-permute-start.3 = (f32[64,2048]{1,0:T(8,128)}, f32[64,2048]{1,0:T(8,128)S(1)}, u32[]{:S(2)}, u32[]{:S(2)}) collective-permute-start(f32[64,2048]{1,0:T(8,128)} %get-tuple-element.37), channel_id=1, source_target_pairs={{0,1},{1,2},{2,3},{3,4},{4,5},{5,6},{6,7},{7,8},{8,9},{9,10},{10,1... | collective-permute-start | bytes 1572872 | tf_op jit(solution)/shard_map/ppermute | solution.py:21
  26.1 1.3 %collective-permute-start.2 = (f32[1,2048]{1,0:T(1,128)S(1)}, f32[1,2048]{1,0:T(1,128)S(1)}, u32[]{:S(2)}, u32[]{:S(2)}) collective-permute-start(f32[1,2048]{1,0:T(1,128)S(1)} %slice.36), channel_id=1, source_target_pairs={{2,0},{3,1},{4,2},{5,3},{6,4},{7,5},{8,6},{9,7},{10,8},{11,9},{12,... | collective-permute-start | bytes 24584 | tf_op jit(solution)/shard_map/ppermute | solution.py:21
  27.4 0.1 pad_add_fusion.place
  27.5 10.1 %collective-permute-done.2.far = f32[1,2048]{1,0:T(1,128)S(1)} collective-permute-done((f32[1,2048]{1,0:T(1,128)S(1)}, f32[1,2048]{1,0:T(1,128)S(1)}, u32[]{:S(2)}, u32[]{:S(2)}) %collective-permute-start.2) | collective-permute-done | bytes 8224 | tf_op jit(solution)/shard_map/ppermute | solution.py:21
  37.6 4.9 %shard_map.105 = (f32[32,2,128]{2,1,0:T(2,128)S(1)}, f32[11,2,8,2048]{3,2,1,0:T(8,128)S(1)}, f32[9,2,8,2048]{3,2,1,0:T(8,128)S(1)}, f32[7,2,8,2048]{3,2,1,0:T(8,...) custom-call(f32[32,256]{1,0:T(8,128)S(1)} %get-tuple-element.19._.ea, ...), custom_call_target="tpu_custom_call" | custom-call | tf_op jit(solution)/shard_map/pallas_call | solution.py:551
  42.4 12.7 %all_to_all.10.got = f32[32,2,128]{2,1,0:T(2,128)S(1)} all-to-all(f32[32,2,128]{2,1,0:T(2,128)S(1)} %get-tuple-element.20), channel_id=1, replica_groups=mesh['rows'=32] {'rows'}, dimensions={0} | all-to-all | bytes 65536 | tf_op jit(solution)/shard_map/all_to_all | solution.py:25
  55.1 0.0 collective-permute-done.4.far_after
  55.1 0.0 collective-permute-done.3.far_before
  55.1 0.0 copy-start.8
  55.2 7.2 %shard_map.106 = (f32[32,2,128]{2,1,0:T(2,128)S(1)}, f32[4,4,2,8,2048]{4,3,2,1,0:T(8,128)S(1)}, f32[4,2,8,2048]{3,2,1,0:T(8,128)S(1)}) custom-call(s32[2]{0:T(128)S(1)} %pad_add_fusion.place, f32[32,2,128]{2,1,0:T(2,128)S(1)} %all_to_all.10.got, f32[11,2,8,2048]{3,2,1,0:T(8,128)S(1)} %get-tuple-element.21.f0, f32[9,2,8,2048]{3,2,1,0:T(8,128)S(1)} %get-tuple-element.22.f1, ...), custom_call_target="tpu_custom_call" | custom-call | tf_op jit(solution)/shard_map/pallas_call | solution.py:551
  62.3 9.0 %all_to_all.11.got = f32[32,2,128]{2,1,0:T(2,128)S(1)} all-to-all(f32[32,2,128]{2,1,0:T(2,128)S(1)} %get-tuple-element.30), channel_id=1, replica_groups=mesh['rows'=32] {'rows'}, dimensions={0} | all-to-all | bytes 65536 | tf_op jit(solution)/shard_map/all_to_all | solution.py:25
  71.3 0.0 copy-done.1
  71.3 2.3 %shard_map.107 = f32[32,256]{1,0:T(8,128)S(1)} custom-call(f32[32,2,128]{2,1,0:T(2,128)S(1)} %all_to_all.11.got, f32[4,4,2,8,2048]{4,3,2,1,0:T(8,128)S(1)} %get-tuple-element.31.kept, f32[4,2,8,2048]{3,2,1,0:T(8,128)S(1)} %get-tuple-element.32.state, f32[72,2048]{1,0:T(8,128)S(1)} %pad_maximum_fusion.4.own.log, bf16[1024,2048]{1,0:T(8,128)(2,1)S(1)} %copy-done.1, ...), custom_call_target="tpu_custom_call" | custom-call | tf_op jit(solution)/shard_map/pallas_call | solution.py:551
  73.5 0.1 collective-permute-start.5
  73.7 1.1 %collective-permute-done.5 = f32[32,256]{1,0:T(8,128)S(1)} collective-permute-done((f32[32,256]{1,0:T(8,128)S(1)}, f32[32,256]{1,0:T(8,128)S(1)}, u32[]{:S(2)}, u32[]{:S(2)}) %collective-permute-start.5) | collective-permute-done | bytes 32800 | tf_op jit(solution)/shard_map/ppermute | solution.py:37
  74.8 0.6 collective-permute-start.8
  75.4 1.3 %collective-permute-start.7 = (f32[32,256]{1,0:T(8,128)S(1)}, f32[32,256]{1,0:T(8,128)S(1)}, u32[]{:S(2)}, u32[]{:S(2)}) collective-permute-start(f32[32,256]{1,0:T(8,128)S(1)} %add.21), channel_id=1, source_target_pairs={{0,4},{1,5},{2,6},{3,7},{4,0},{5,1},{6,2},{7,3},{8,12},{9,13},{10,... | collective-permute-start | bytes 98312 | tf_op jit(solution)/shard_map/ppermute | solution.py:37
  76.7 1.5 %collective-permute-start.6 = (f32[32,256]{1,0:T(8,128)S(1)}, f32[32,256]{1,0:T(8,128)S(1)}, u32[]{:S(2)}, u32[]{:S(2)}) collective-permute-start(f32[32,256]{1,0:T(8,128)S(1)} %add.21), channel_id=1, source_target_pairs={{0,2},{1,3},{2,0},{3,1},{4,6},{5,7},{6,4},{7,5},{8,10},{9,11},{10,... | collective-permute-start | bytes 98312 | tf_op jit(solution)/shard_map/ppermute | solution.py:37
  78.3 1.5 %collective-permute-done.8 = f32[32,256]{1,0:T(8,128)S(1)} collective-permute-done((f32[32,256]{1,0:T(8,128)S(1)}, f32[32,256]{1,0:T(8,128)S(1)}, u32[]{:S(2)}, u32[]{:S(2)}) %collective-permute-start.8) | collective-permute-done | bytes 32800 | tf_op jit(solution)/shard_map/ppermute | solution.py:37
  79.8 0.0 collective-permute-done.7
  79.8 0.9 collective-permute-done.6
  80.7 0.6 collective-permute-start.11
  81.3 1.5 %collective-permute-start.10 = (f32[32,256]{1,0:T(8,128)S(1)}, f32[32,256]{1,0:T(8,128)S(1)}, u32[]{:S(2)}, u32[]{:S(2)}) collective-permute-start(f32[32,256]{1,0:T(8,128)S(1)} %add_add_fusion.1), channel_id=1, source_target_pairs={{0,16},{1,17},{2,18},{3,19},{4,20},{5,21},{6,22},{7,23},{8,24},{9,... | collective-permute-start | bytes 98312 | tf_op jit(solution)/shard_map/ppermute | solution.py:37
  82.8 2.3 %collective-permute-start.9 = (f32[32,256]{1,0:T(8,128)S(1)}, f32[32,256]{1,0:T(8,128)S(1)}, u32[]{:S(2)}, u32[]{:S(2)}) collective-permute-start(f32[32,256]{1,0:T(8,128)S(1)} %add_add_fusion.1), channel_id=1, source_target_pairs={{0,8},{1,9},{2,10},{3,11},{4,12},{5,13},{6,14},{7,15},{8,0},{9,1},... | collective-permute-start | bytes 98312 | tf_op jit(solution)/shard_map/ppermute | solution.py:37
  85.1 1.3 %collective-permute-done.11 = f32[32,256]{1,0:T(8,128)S(1)} collective-permute-done((f32[32,256]{1,0:T(8,128)S(1)}, f32[32,256]{1,0:T(8,128)S(1)}, u32[]{:S(2)}, u32[]{:S(2)}) %collective-permute-start.11) | collective-permute-done | bytes 32800 | tf_op jit(solution)/shard_map/ppermute | solution.py:37
  86.4 0.0 collective-permute-done.10
  86.4 0.6 collective-permute-done.9
  87.0 0.0 copy-done.3
  87.0 0.0 copy-done.7
  87.0 2.5 %shard_map.108 = (f32[16,4,2048]{2,1,0:T(4,128)}, f32[16,256]{1,0:T(8,128)}) custom-call(f32[32,256]{1,0:T(8,128)S(1)} %add_add_fusion.sums, f32[1,256]{1,0:T(1,128)S(1)} %bitcast.15, f32[16,256]{1,0:T(8,128)S(1)} %copy-done.7, bf16[1024,2048]{1,0:T(8,128)(2,1)S(1)} %copy-done.1, f32[16,4,2048]{2,1,0:T(4,128)S(1)} %copy-done.3, f32[16,4,2048]{2,1,0:T(4,128)S(1)} %copy-done.4), custom_call_target="tpu_custom_call" | custom-call | tf_op jit(solution)/shard_map/pallas_call | solution.py:551
  (20 shorter events, 0.2 us)
Async XLA Ops:
  0.6 1.5 %copy-start.9 = (f32[4,2048]{1,0:T(4,128)S(1)}, f32[4,2048]{1,0:T(4,128)}, u32[]{:S(2)}) copy-start(f32[4,2048]{1,0:T(4,128)} %param.12) | copy-start | bytes 98308
  0.6 1.5 %copy-start.10 = (f32[4,2048]{1,0:T(4,128)S(1)}, f32[4,2048]{1,0:T(4,128)}, u32[]{:S(2)}) copy-start(f32[4,2048]{1,0:T(4,128)} %param.9) | copy-start | bytes 98308
  0.6 6.2 %copy-start.4 = (f32[16,4,2048]{2,1,0:T(4,128)S(1)}, f32[16,4,2048]{2,1,0:T(4,128)}, u32[]{:S(2)}) copy-start(f32[16,4,2048]{2,1,0:T(4,128)} %noise.1) | copy-start | bytes 1572868
  2.1 5.1 %copy-start.2 = (bf16[256,4,2048]{2,1,0:T(4,128)(2,1)S(1)}, bf16[256,4,2048]{2,1,0:T(4,128)(2,1)}, u32[]{:S(2)}) copy-start(bf16[256,4,2048]{2,1,0:T(4,128)(2,1)} %basis.1) | copy-start | bytes 12582916
  2.2 9.0 %collective-permute-start.1 = (f32[72,2048]{1,0:T(8,128)S(1)}, f32[72,2048]{1,0:T(8,128)S(1)}, u32[]{:S(2)}, u32[]{:S(2)}) collective-permute-start(f32[72,2048]{1,0:T(8,128)S(1)} %pad_maximum_fusion.4.own.log), channel_id=1, source_target_pairs={{1,0},{2,1},{3,2},{4,3},{5,4},{6,5},{7,6},{8,7},{9,8},{10,9},{11,1... | collective-permute-start | bytes 1769480 | tf_op jit(solution)/shard_map/ppermute | solution.py:21
  3.8 7.3 %collective-permute-start = (f32[56,2048]{1,0:T(8,128)S(1)}, f32[56,2048]{1,0:T(8,128)S(1)}, u32[]{:S(2)}, u32[]{:S(2)}) collective-permute-start(f32[56,2048]{1,0:T(8,128)S(1)} %slice.43), channel_id=1, source_target_pairs={{0,1},{1,2},{2,3},{3,4},{4,5},{5,6},{6,7},{7,8},{8,9},{9,10},{10,1... | collective-permute-start | bytes 1376264 | tf_op jit(solution)/shard_map/ppermute | solution.py:21
  7.2 4.1 %copy-start.5 = (f32[4,2048]{1,0:T(4,128)S(1)}, f32[4,2048]{1,0:T(4,128)}, u32[]{:S(2)}) copy-start(f32[4,2048]{1,0:T(4,128)} %observed) | copy-start | bytes 98308
  7.2 4.1 %copy-start.6 = (f32[4,2048]{1,0:T(4,128)S(1)}, f32[4,2048]{1,0:T(4,128)}, u32[]{:S(2)}) copy-start(f32[4,2048]{1,0:T(4,128)} %precision) | copy-start | bytes 98308
  9.2 2.0 %copy-start = (bf16[1024,2048]{1,0:T(8,128)(2,1)}, bf16[1024,2048]{1,0:T(8,128)(2,1)S(1)}, u32[]{:S(2)}) copy-start(bf16[1024,2048]{1,0:T(8,128)(2,1)S(1)} %get-tuple-element.33.fields) | copy-start | bytes 12582916
  12.3 42.8 %collective-permute-start.4 = (f32[64,2048]{1,0:T(8,128)}, f32[64,2048]{1,0:T(8,128)S(1)}, u32[]{:S(2)}, u32[]{:S(2)}) collective-permute-start(f32[64,2048]{1,0:T(8,128)} %get-tuple-element.36), channel_id=1, source_target_pairs={{1,0},{2,1},{3,2},{4,3},{5,4},{6,5},{7,6},{8,7},{9,8},{10,9},{11,1... | collective-permute-start | bytes 1572872 | tf_op jit(solution)/shard_map/ppermute | solution.py:21
  13.6 41.5 %collective-permute-start.3 = (f32[64,2048]{1,0:T(8,128)}, f32[64,2048]{1,0:T(8,128)S(1)}, u32[]{:S(2)}, u32[]{:S(2)}) collective-permute-start(f32[64,2048]{1,0:T(8,128)} %get-tuple-element.37), channel_id=1, source_target_pairs={{0,1},{1,2},{2,3},{3,4},{4,5},{5,6},{6,7},{7,8},{8,9},{9,10},{10,1... | collective-permute-start | bytes 1572872 | tf_op jit(solution)/shard_map/ppermute | solution.py:21
  26.1 11.5 %collective-permute-start.2 = (f32[1,2048]{1,0:T(1,128)S(1)}, f32[1,2048]{1,0:T(1,128)S(1)}, u32[]{:S(2)}, u32[]{:S(2)}) collective-permute-start(f32[1,2048]{1,0:T(1,128)S(1)} %slice.36), channel_id=1, source_target_pairs={{2,0},{3,1},{4,2},{5,3},{6,4},{7,5},{8,6},{9,7},{10,8},{11,9},{12,... | collective-permute-start | bytes 24584 | tf_op jit(solution)/shard_map/ppermute | solution.py:21
  55.1 16.1 %copy-start.1 = (bf16[1024,2048]{1,0:T(8,128)(2,1)S(1)}, bf16[1024,2048]{1,0:T(8,128)(2,1)}, u32[]{:S(2)}) copy-start(bf16[1024,2048]{1,0:T(8,128)(2,1)} %copy-done) | copy-start | bytes 12582916
  55.1 16.1 %copy-start.8 = (f32[256]{0:T(256)S(1)}, f32[256]{0:T(256)}, u32[]{:S(2)}) copy-start(f32[256]{0:T(256)} %param.16) | copy-start | bytes 3076
  71.3 15.7 %copy-start.3 = (f32[16,4,2048]{2,1,0:T(4,128)S(1)}, f32[16,4,2048]{2,1,0:T(4,128)}, u32[]{:S(2)}) copy-start(f32[16,4,2048]{2,1,0:T(4,128)} %log.1) | copy-start | bytes 1572868
  71.3 15.7 %copy-start.7 = (f32[16,256]{1,0:T(8,128)S(1)}, f32[16,256]{1,0:T(8,128)}, u32[]{:S(2)}) copy-start(f32[16,256]{1,0:T(8,128)} %subspace.1) | copy-start | bytes 49156
  73.5 1.2 %collective-permute-start.5 = (f32[32,256]{1,0:T(8,128)S(1)}, f32[32,256]{1,0:T(8,128)S(1)}, u32[]{:S(2)}, u32[]{:S(2)}) collective-permute-start(f32[32,256]{1,0:T(8,128)S(1)} %shard_map.107), channel_id=1, source_target_pairs={{0,1},{1,0},{2,3},{3,2},{4,5},{5,4},{6,7},{7,6},{8,9},{9,8},{10,11... | collective-permute-start | bytes 98312 | tf_op jit(solution)/shard_map/ppermute | solution.py:37
  74.8 5.0 %collective-permute-start.8 = (f32[32,256]{1,0:T(8,128)S(1)}, f32[32,256]{1,0:T(8,128)S(1)}, u32[]{:S(2)}, u32[]{:S(2)}) collective-permute-start(f32[32,256]{1,0:T(8,128)S(1)} %add.21), channel_id=1, source_target_pairs={{0,6},{1,7},{2,4},{3,5},{4,2},{5,3},{6,0},{7,1},{8,14},{9,15},{10,... | collective-permute-start | bytes 98312 | tf_op jit(solution)/shard_map/ppermute | solution.py:37
  75.4 4.4 %collective-permute-start.7 = (f32[32,256]{1,0:T(8,128)S(1)}, f32[32,256]{1,0:T(8,128)S(1)}, u32[]{:S(2)}, u32[]{:S(2)}) collective-permute-start(f32[32,256]{1,0:T(8,128)S(1)} %add.21), channel_id=1, source_target_pairs={{0,4},{1,5},{2,6},{3,7},{4,0},{5,1},{6,2},{7,3},{8,12},{9,13},{10,... | collective-permute-start | bytes 98312 | tf_op jit(solution)/shard_map/ppermute | solution.py:37
  76.7 3.9 %collective-permute-start.6 = (f32[32,256]{1,0:T(8,128)S(1)}, f32[32,256]{1,0:T(8,128)S(1)}, u32[]{:S(2)}, u32[]{:S(2)}) collective-permute-start(f32[32,256]{1,0:T(8,128)S(1)} %add.21), channel_id=1, source_target_pairs={{0,2},{1,3},{2,0},{3,1},{4,6},{5,7},{6,4},{7,5},{8,10},{9,11},{10,... | collective-permute-start | bytes 98312 | tf_op jit(solution)/shard_map/ppermute | solution.py:37
  80.7 5.8 %collective-permute-start.11 = (f32[32,256]{1,0:T(8,128)S(1)}, f32[32,256]{1,0:T(8,128)S(1)}, u32[]{:S(2)}, u32[]{:S(2)}) collective-permute-start(f32[32,256]{1,0:T(8,128)S(1)} %add_add_fusion.1), channel_id=1, source_target_pairs={{0,24},{1,25},{2,26},{3,27},{4,28},{5,29},{6,30},{7,31},{8,16},{9,... | collective-permute-start | bytes 98312 | tf_op jit(solution)/shard_map/ppermute | solution.py:37
  81.3 5.2 %collective-permute-start.10 = (f32[32,256]{1,0:T(8,128)S(1)}, f32[32,256]{1,0:T(8,128)S(1)}, u32[]{:S(2)}, u32[]{:S(2)}) collective-permute-start(f32[32,256]{1,0:T(8,128)S(1)} %add_add_fusion.1), channel_id=1, source_target_pairs={{0,16},{1,17},{2,18},{3,19},{4,20},{5,21},{6,22},{7,23},{8,24},{9,... | collective-permute-start | bytes 98312 | tf_op jit(solution)/shard_map/ppermute | solution.py:37
  82.8 4.2 %collective-permute-start.9 = (f32[32,256]{1,0:T(8,128)S(1)}, f32[32,256]{1,0:T(8,128)S(1)}, u32[]{:S(2)}, u32[]{:S(2)}) collective-permute-start(f32[32,256]{1,0:T(8,128)S(1)} %add_add_fusion.1), channel_id=1, source_target_pairs={{0,8},{1,9},{2,10},{3,11},{4,12},{5,13},{6,14},{7,15},{8,0},{9,1},... | collective-permute-start | bytes 98312 | tf_op jit(solution)/shard_map/ppermute | solution.py:37

commit v2 on v1

--- a/solution.py
+++ b/solution.py
@@ -106,7 +106,7 @@
     return folds
 
 
-def krylov(vectors, images, inverse, across, along):
+def krylov(rows, vectors, images, inverse, across, along):
     width = across.shape[-1]
     groups = inverse.shape[1]
     for k in range(ITERS - 1):
@@ -117,7 +117,8 @@
                 side = across[at]
                 beside = pltpu.roll(side * v, 1, 1) + side * pltpu.roll(v, width - 1, 1)
                 image = along[at] * vectors[k][i, g] + along[at + 1] * vectors[k][i + 2, g] + beside
-                images[k][i, g] = image
+                if 0 <= i + k + 2 - ITERS < rows:
+                    images[k][i, g] = image
                 vectors[k + 1][i, g] = image * inverse[at, g]
 
 
@@ -264,7 +265,7 @@
                 value = jnp.where(outside, 0.0, value)
             inverse[i, g] = value
             vectors[0][i, g] = source * value
-    krylov(vectors, images, inverse, across, along)
+    krylov(rows, vectors, images, inverse, across, along)
     tile = moment_tile(
         rows, lambda r, g, cut: side[r, :, cut], vectors, images, thirds, halves, across, along
     )
@@ -304,7 +305,10 @@
     precision,
     observed,
     sent,
-    kept,
+    w0,
+    w1,
+    w2,
+    w3,
     state,
     side,
     outer,
@@ -396,7 +400,7 @@
                 image = along_at(row) * vector(k, row - 1, g) + along_at(row + 1) * vector(k, row + 1, g) + image
                 outer[k + 1, i, g] = image * inverse_at(row, g)
 
-    vectors, images = scratch[:ITERS], scratch[ITERS:]
+    vectors, images = (w0, w1, w2, w3), scratch
     tile = total_of(got)
     for g in range(groups):
         weights = weights_of(tile, g)
@@ -419,15 +423,11 @@
             if 0 <= row < rows:
                 side[row, g] = value
             vectors[0][i, g] = value * inverse[i, g]
-    krylov(vectors, images, inverse, across, along)
+    krylov(rows, vectors, images, inverse, across, along)
     tile = moment_tile(
         rows, lambda r, g, cut: side[r, g, :, cut], vectors, images, thirds, halves, across, along
     )
     sent[...] = jnp.broadcast_to(tile[None], sent.shape)
-    for k in range(ITERS):
-        for r in range(rows):
-            for g in range(groups):
-                kept[k, r, g] = vectors[k][r + above - k, g]
 
 
 def factors(eigenvalues):
@@ -480,7 +480,7 @@
 
 
 def gradient_kernel(
-    got, kept, state, log, fields, early, eigenvalues, sums, gradient, picked, *, rows, groups
+    got, w0, w1, w2, w3, state, log, fields, early, eigenvalues, sums, gradient, picked, *, rows, groups
 ):
     tile = total_of(got)
     chains = groups * SUB
@@ -488,9 +488,9 @@
     for g in range(groups):
         weights = weights_of(tile, g)
         for r in range(rows):
-            value = weights[0] * kept[0, r, g]
+            value = weights[0] * w0[r + ITERS - 1, g]
             for k in range(1, ITERS):
-                value = value + weights[k] * kept[k, r, g]
+                value = value + weights[k] * (w0, w1, w2, w3)[k][r + ITERS - 1 - k, g]
             at = spot.log(r, g)
             value = -jnp.exp(log[at : at + SUB, :]) * value * state[r, g]
             at = r * chains + g * SUB
@@ -624,9 +624,9 @@
         rows=rows,
         groups=groups,
     )
-    sent, kept, state = call(
+    sent, *solved, state = call(
         adjoint_kernel,
-        [tiles, (ITERS, rows) + block, (rows,) + block],
+        [tiles] + frames + [(rows,) + block],
         [place, exchanged(sent), *vectors, inverse, across, along]
         + [before, after, far_before, far_after, precision, observed],
         [
@@ -637,7 +637,6 @@
             (6, SUB, width),
         ]
         + moments
-        + frames
         + images,
         spaces={0: pltpu.SMEM},
         rows=rows,
@@ -646,7 +645,7 @@
     (sums,) = call(
         gradient_kernel,
         [(2 * chains, rank)],
-        [exchanged(sent), kept, state, packed, fields, early, eigenvalues[None]],
+        [exchanged(sent), *solved, state, packed, fields, early, eigenvalues[None]],
         [(rows * chains, width), (chains, rows * rank)],
         rows=rows,
         groups=groups,

time: 89.9 us -> 89.8 us (level)
  transfers between devices with their start and end apart: 12 -> 12, of which waited for: 6 -> 6; matrix products, arithmetic and copies ran while one was open for 0% -> 0% of each run, Pallas kernels for 8% -> 7%
where the time goes in v2:
time: 89.8 us; the launch traced here: 89.5 us
  starting transfers between devices  27.1 us (30%)
  blocking collectives  21.6 us (24%)
  Pallas kernels  18.6 us (21%)
  waiting for transfers between devices  15.5 us (17%)
  local copies, waits for them, and re-layouts  4.36 us (5%)
  other arithmetic  1.32 us (1%)
  between operations  1.06 us (1%)
    all_to_all x2, blocking collectives, exchanged(): return lax.all_to_all(value, AXIS, 0, 0)  21.6 us
    ppermute x5, starting transfers between devices, shifted(): return lax.ppermute(value, AXIS, pairs)  19 us
    pallas_call x5, Pallas kernels, call(): pl.pallas_call(functools.partial(kernel, **static), out_shape=[jax.ShapeD...  18.6 us
    ppermute x5, waiting for transfers between devices, shifted(): return lax.ppermute(value, AXIS, pairs)  10.1 us
    ppermute x7, starting transfers between devices, summed(): lax.ppermute(value, AXIS, [(i, i ^ k * stride) for i in range(count)])  8.06 us
    ppermute x7, waiting for transfers between devices, summed(): lax.ppermute(value, AXIS, [(i, i ^ k * stride) for i in range(count)])  5.37 us
    unnamed x23, local copies, waits for them, and re-layouts  4.07 us
  transfers between devices with their start and end apart: 12, of which 6 were waited for; matrix products, arithmetic and copies ran while one was open for 0% of the time, Pallas kernels for 7%

profile of v2, /device:TPU:0, one launch (start us, length us, event | category | flops | bytes accessed | tf_op | source)
XLA Modules:
  0.0 89.5 jit_solution(13845201950635433184)
XLA Ops:
  0.6 0.0 copy-start.9
  0.6 0.0 copy-start.10
  0.7 1.4 %copy.14 = f32[16,4,2048]{2,0,1:T(8,128)S(1)} copy(f32[16,4,2048]{2,1,0:T(4,128)} %log.1) | data formatting | bytes 1048576 | tf_op args[4]
  2.1 0.0 copy-start.2
  2.1 0.0 copy-done.9
  2.1 0.0 copy-done.10
  2.2 1.6 %collective-permute-start.1 = (f32[72,2048]{1,0:T(8,128)S(1)}, f32[72,2048]{1,0:T(8,128)S(1)}, u32[]{:S(2)}, u32[]{:S(2)}) collective-permute-start(f32[72,2048]{1,0:T(8,128)S(1)} %pad_maximum_fusion.4.own.log), channel_id=1, source_target_pairs={{1,0},{2,1},{3,2},{4,3},{5,4},{6,5},{7,6},{8,7},{9,8},{10,9},{11,1... | collective-permute-start | bytes 1769480 | tf_op jit(solution)/shard_map/ppermute | solution.py:21
  3.8 3.1 %collective-permute-start = (f32[56,2048]{1,0:T(8,128)S(1)}, f32[56,2048]{1,0:T(8,128)S(1)}, u32[]{:S(2)}, u32[]{:S(2)}) collective-permute-start(f32[56,2048]{1,0:T(8,128)S(1)} %slice.43), channel_id=1, source_target_pairs={{0,1},{1,2},{2,3},{3,4},{4,5},{5,6},{6,7},{7,8},{8,9},{9,10},{10,1... | collective-permute-start | bytes 1376264 | tf_op jit(solution)/shard_map/ppermute | solution.py:21
  6.9 0.1 convert_bitcast_fusion
  7.0 0.2 copy.12
  7.2 0.0 copy-done.2
  7.2 2.0 %shard_map.104 = (bf16[1024,2048]{1,0:T(8,128)(2,1)S(1)}, f32[32,256]{1,0:T(8,128)S(1)}) custom-call(bf16[256,4,2048]{2,1,0:T(4,128)(2,1)S(1)} %copy-done.2, f32[72,2048]{1,0:T(8,128)S(1)} %pad_maximum_fusion.4.own.log, bf16[64,2048]{1,0:T(8,128)(2,1)S(1)} %bitcast.13), custom_call_target="tpu_custom_call" | custom-call | tf_op jit(solution)/shard_map/pallas_call | solution.py:551
  9.1 2.0 %copy-done = bf16[1024,2048]{1,0:T(8,128)(2,1)} copy-done((bf16[1024,2048]{1,0:T(8,128)(2,1)}, bf16[1024,2048]{1,0:T(8,128)(2,1)S(1)}, u32[]{:S(2)}) %copy-start) | copy-done | bytes 4194328
  11.1 0.0 collective-permute-done.before
  11.2 0.0 collective-permute-done.1.after
  11.2 0.6 copy-done.5
  11.9 0.0 copy-done.6
  11.9 1.1 %pad_maximum_fusion = (f32[64,2048]{1,0:T(8,128)}, f32[64,2048]{1,0:T(8,128)}) fusion(f32[4,2048]{1,0:T(4,128)S(1)} %copy-done.5, f32[4,2048]{1,0:T(4,128)S(1)} %copy-done.6, f32[56,2048]{1,0:T(8,128)S(1)} %slice.46, f32[16,2048]{1,0:T(8,128)S(1)} %slice_bitcast_fusion, f32[40,2048]{1,0:T(8,128)S(1)} %slice.44), kind=kLoop, calls=%fused_computation | loop fusion | flops 655360 | bytes 2031616 | tf_op jit(solution)/shard_map/concatenate | solution.py:608
  12.9 1.3 %collective-permute-start.4 = (f32[64,2048]{1,0:T(8,128)}, f32[64,2048]{1,0:T(8,128)S(1)}, u32[]{:S(2)}, u32[]{:S(2)}) collective-permute-start(f32[64,2048]{1,0:T(8,128)} %get-tuple-element.42), channel_id=1, source_target_pairs={{1,0},{2,1},{3,2},{4,3},{5,4},{6,5},{7,6},{8,7},{9,8},{10,9},{11,1... | collective-permute-start | bytes 1572872 | tf_op jit(solution)/shard_map/ppermute | solution.py:21
  14.2 11.8 %collective-permute-start.3 = (f32[64,2048]{1,0:T(8,128)}, f32[64,2048]{1,0:T(8,128)S(1)}, u32[]{:S(2)}, u32[]{:S(2)}) collective-permute-start(f32[64,2048]{1,0:T(8,128)} %get-tuple-element.43), channel_id=1, source_target_pairs={{0,1},{1,2},{2,3},{3,4},{4,5},{5,6},{6,7},{7,8},{8,9},{9,10},{10,1... | collective-permute-start | bytes 1572872 | tf_op jit(solution)/shard_map/ppermute | solution.py:21
  26.1 1.3 %collective-permute-start.2 = (f32[1,2048]{1,0:T(1,128)S(1)}, f32[1,2048]{1,0:T(1,128)S(1)}, u32[]{:S(2)}, u32[]{:S(2)}) collective-permute-start(f32[1,2048]{1,0:T(1,128)S(1)} %slice.36), channel_id=1, source_target_pairs={{2,0},{3,1},{4,2},{5,3},{6,4},{7,5},{8,6},{9,7},{10,8},{11,9},{12,... | collective-permute-start | bytes 24584 | tf_op jit(solution)/shard_map/ppermute | solution.py:21
  27.4 0.1 pad_add_fusion.place
  27.5 10.1 %collective-permute-done.2.far = f32[1,2048]{1,0:T(1,128)S(1)} collective-permute-done((f32[1,2048]{1,0:T(1,128)S(1)}, f32[1,2048]{1,0:T(1,128)S(1)}, u32[]{:S(2)}, u32[]{:S(2)}) %collective-permute-start.2) | collective-permute-done | bytes 8224 | tf_op jit(solution)/shard_map/ppermute | solution.py:21
  37.6 4.7 %shard_map.105 = (f32[32,2,128]{2,1,0:T(2,128)S(1)}, f32[11,2,8,2048]{3,2,1,0:T(8,128)S(1)}, f32[9,2,8,2048]{3,2,1,0:T(8,128)S(1)}, f32[7,2,8,2048]{3,2,1,0:T(8,...) custom-call(f32[32,256]{1,0:T(8,128)S(1)} %get-tuple-element.22._.ea, ...), custom_call_target="tpu_custom_call" | custom-call | tf_op jit(solution)/shard_map/pallas_call | solution.py:551
  42.3 12.7 %all_to_all.10.got = f32[32,2,128]{2,1,0:T(2,128)S(1)} all-to-all(f32[32,2,128]{2,1,0:T(2,128)S(1)} %get-tuple-element.23), channel_id=1, replica_groups=mesh['rows'=32] {'rows'}, dimensions={0} | all-to-all | bytes 65536 | tf_op jit(solution)/shard_map/all_to_all | solution.py:25
  55.0 0.0 collective-permute-done.4.far_after
  55.0 0.0 collective-permute-done.3.far_before
  55.0 0.0 copy-start.8
  55.0 7.1 %shard_map.106 = (f32[32,2,128]{2,1,0:T(2,128)S(1)}, f32[11,2,8,2048]{3,2,1,0:T(8,128)S(1)}, f32[9,2,8,2048]{3,2,1,0:T(8,128)S(1)}, f32[7,2,8,2048]{3,2,1,0:T(8,...) custom-call(s32[2]{0:T(128)S(1)} %pad_add_fusion.place, f32[32,2,128]{2,1,0:T(2,128)S(1)} %all_to_all.10.got, ...), custom_call_target="tpu_custom_call" | custom-call | tf_op jit(solution)/shard_map/pallas_call | solution.py:551
  62.1 9.0 %all_to_all.11.got = f32[32,2,128]{2,1,0:T(2,128)S(1)} all-to-all(f32[32,2,128]{2,1,0:T(2,128)S(1)} %get-tuple-element.33), channel_id=1, replica_groups=mesh['rows'=32] {'rows'}, dimensions={0} | all-to-all | bytes 65536 | tf_op jit(solution)/shard_map/all_to_all | solution.py:25
  71.1 2.3 %shard_map.107 = f32[32,256]{1,0:T(8,128)S(1)} custom-call(f32[32,2,128]{2,1,0:T(2,128)S(1)} %all_to_all.11.got, f32[11,2,8,2048]{3,2,1,0:T(8,128)S(1)} %get-tuple-element.34.w0, f32[9,2,8,2048]{3,2,1,0:T(8,128)S(1)} %get-tuple-element.35.w1, f32[7,2,8,2048]{3,2,1,0:T(8,128)S(1)} %get-tuple-element.36.w2, f32[5,2,8,2048]{3,2,1,0:T(8,128)S(1)} %get-tuple-element.37.w3, ...), custom_call_target="tpu_custom_call" | custom-call | tf_op jit(solution)/shard_map/pallas_call | solution.py:551
  73.4 0.1 collective-permute-start.5
  73.5 1.1 %collective-permute-done.5 = f32[32,256]{1,0:T(8,128)S(1)} collective-permute-done((f32[32,256]{1,0:T(8,128)S(1)}, f32[32,256]{1,0:T(8,128)S(1)}, u32[]{:S(2)}, u32[]{:S(2)}) %collective-permute-start.5) | collective-permute-done | bytes 32800 | tf_op jit(solution)/shard_map/ppermute | solution.py:37
  74.6 0.6 collective-permute-start.8
  75.2 1.3 %collective-permute-start.7 = (f32[32,256]{1,0:T(8,128)S(1)}, f32[32,256]{1,0:T(8,128)S(1)}, u32[]{:S(2)}, u32[]{:S(2)}) collective-permute-start(f32[32,256]{1,0:T(8,128)S(1)} %add.21), channel_id=1, source_target_pairs={{0,4},{1,5},{2,6},{3,7},{4,0},{5,1},{6,2},{7,3},{8,12},{9,13},{10,... | collective-permute-start | bytes 98312 | tf_op jit(solution)/shard_map/ppermute | solution.py:37
  76.5 1.5 %collective-permute-start.6 = (f32[32,256]{1,0:T(8,128)S(1)}, f32[32,256]{1,0:T(8,128)S(1)}, u32[]{:S(2)}, u32[]{:S(2)}) collective-permute-start(f32[32,256]{1,0:T(8,128)S(1)} %add.21), channel_id=1, source_target_pairs={{0,2},{1,3},{2,0},{3,1},{4,6},{5,7},{6,4},{7,5},{8,10},{9,11},{10,... | collective-permute-start | bytes 98312 | tf_op jit(solution)/shard_map/ppermute | solution.py:37
  78.1 1.5 %collective-permute-done.8 = f32[32,256]{1,0:T(8,128)S(1)} collective-permute-done((f32[32,256]{1,0:T(8,128)S(1)}, f32[32,256]{1,0:T(8,128)S(1)}, u32[]{:S(2)}, u32[]{:S(2)}) %collective-permute-start.8) | collective-permute-done | bytes 32800 | tf_op jit(solution)/shard_map/ppermute | solution.py:37
  79.6 0.0 collective-permute-done.7
  79.6 0.9 collective-permute-done.6
  80.5 0.6 collective-permute-start.11
  81.1 1.5 %collective-permute-start.10 = (f32[32,256]{1,0:T(8,128)S(1)}, f32[32,256]{1,0:T(8,128)S(1)}, u32[]{:S(2)}, u32[]{:S(2)}) collective-permute-start(f32[32,256]{1,0:T(8,128)S(1)} %add_add_fusion.1), channel_id=1, source_target_pairs={{0,16},{1,17},{2,18},{3,19},{4,20},{5,21},{6,22},{7,23},{8,24},{9,... | collective-permute-start | bytes 98312 | tf_op jit(solution)/shard_map/ppermute | solution.py:37
  82.6 2.3 %collective-permute-start.9 = (f32[32,256]{1,0:T(8,128)S(1)}, f32[32,256]{1,0:T(8,128)S(1)}, u32[]{:S(2)}, u32[]{:S(2)}) collective-permute-start(f32[32,256]{1,0:T(8,128)S(1)} %add_add_fusion.1), channel_id=1, source_target_pairs={{0,8},{1,9},{2,10},{3,11},{4,12},{5,13},{6,14},{7,15},{8,0},{9,1},... | collective-permute-start | bytes 98312 | tf_op jit(solution)/shard_map/ppermute | solution.py:37
  84.9 1.3 %collective-permute-done.11 = f32[32,256]{1,0:T(8,128)S(1)} collective-permute-done((f32[32,256]{1,0:T(8,128)S(1)}, f32[32,256]{1,0:T(8,128)S(1)}, u32[]{:S(2)}, u32[]{:S(2)}) %collective-permute-start.11) | collective-permute-done | bytes 32800 | tf_op jit(solution)/shard_map/ppermute | solution.py:37
  86.3 0.0 collective-permute-done.10
  86.3 0.6 collective-permute-done.9
  86.8 0.0 copy-done.3
  86.8 0.0 copy-done.7
  86.9 2.5 %shard_map.108 = (f32[16,4,2048]{2,1,0:T(4,128)}, f32[16,256]{1,0:T(8,128)}) custom-call(f32[32,256]{1,0:T(8,128)S(1)} %add_add_fusion.sums, f32[1,256]{1,0:T(1,128)S(1)} %bitcast.15, f32[16,256]{1,0:T(8,128)S(1)} %copy-done.7, bf16[1024,2048]{1,0:T(8,128)(2,1)S(1)} %copy-done.1, f32[16,4,2048]{2,1,0:T(4,128)S(1)} %copy-done.3, f32[16,4,2048]{2,1,0:T(4,128)S(1)} %copy-done.4), custom_call_target="tpu_custom_call" | custom-call | tf_op jit(solution)/shard_map/pallas_call | solution.py:551
  (20 shorter events, 0.2 us)
Async XLA Ops:
  0.6 1.5 %copy-start.9 = (f32[4,2048]{1,0:T(4,128)S(1)}, f32[4,2048]{1,0:T(4,128)}, u32[]{:S(2)}) copy-start(f32[4,2048]{1,0:T(4,128)} %param.12) | copy-start | bytes 98308
  0.6 1.5 %copy-start.10 = (f32[4,2048]{1,0:T(4,128)S(1)}, f32[4,2048]{1,0:T(4,128)}, u32[]{:S(2)}) copy-start(f32[4,2048]{1,0:T(4,128)} %param.9) | copy-start | bytes 98308
  0.6 6.2 %copy-start.4 = (f32[16,4,2048]{2,1,0:T(4,128)S(1)}, f32[16,4,2048]{2,1,0:T(4,128)}, u32[]{:S(2)}) copy-start(f32[16,4,2048]{2,1,0:T(4,128)} %noise.1) | copy-start | bytes 1572868
  2.1 5.1 %copy-start.2 = (bf16[256,4,2048]{2,1,0:T(4,128)(2,1)S(1)}, bf16[256,4,2048]{2,1,0:T(4,128)(2,1)}, u32[]{:S(2)}) copy-start(bf16[256,4,2048]{2,1,0:T(4,128)(2,1)} %basis.1) | copy-start | bytes 12582916
  2.2 9.0 %collective-permute-start.1 = (f32[72,2048]{1,0:T(8,128)S(1)}, f32[72,2048]{1,0:T(8,128)S(1)}, u32[]{:S(2)}, u32[]{:S(2)}) collective-permute-start(f32[72,2048]{1,0:T(8,128)S(1)} %pad_maximum_fusion.4.own.log), channel_id=1, source_target_pairs={{1,0},{2,1},{3,2},{4,3},{5,4},{6,5},{7,6},{8,7},{9,8},{10,9},{11,1... | collective-permute-start | bytes 1769480 | tf_op jit(solution)/shard_map/ppermute | solution.py:21
  3.8 7.3 %collective-permute-start = (f32[56,2048]{1,0:T(8,128)S(1)}, f32[56,2048]{1,0:T(8,128)S(1)}, u32[]{:S(2)}, u32[]{:S(2)}) collective-permute-start(f32[56,2048]{1,0:T(8,128)S(1)} %slice.43), channel_id=1, source_target_pairs={{0,1},{1,2},{2,3},{3,4},{4,5},{5,6},{6,7},{7,8},{8,9},{9,10},{10,1... | collective-permute-start | bytes 1376264 | tf_op jit(solution)/shard_map/ppermute | solution.py:21
  9.1 2.0 %copy-start = (bf16[1024,2048]{1,0:T(8,128)(2,1)}, bf16[1024,2048]{1,0:T(8,128)(2,1)S(1)}, u32[]{:S(2)}) copy-start(bf16[1024,2048]{1,0:T(8,128)(2,1)S(1)} %get-tuple-element.39.fields) | copy-start | bytes 12582916
  11.1 0.8 copy-start.5
  11.1 0.8 copy-start.6
  12.9 42.1 %collective-permute-start.4 = (f32[64,2048]{1,0:T(8,128)}, f32[64,2048]{1,0:T(8,128)S(1)}, u32[]{:S(2)}, u32[]{:S(2)}) collective-permute-start(f32[64,2048]{1,0:T(8,128)} %get-tuple-element.42), channel_id=1, source_target_pairs={{1,0},{2,1},{3,2},{4,3},{5,4},{6,5},{7,6},{8,7},{9,8},{10,9},{11,1... | collective-permute-start | bytes 1572872 | tf_op jit(solution)/shard_map/ppermute | solution.py:21
  14.2 40.8 %collective-permute-start.3 = (f32[64,2048]{1,0:T(8,128)}, f32[64,2048]{1,0:T(8,128)S(1)}, u32[]{:S(2)}, u32[]{:S(2)}) collective-permute-start(f32[64,2048]{1,0:T(8,128)} %get-tuple-element.43), channel_id=1, source_target_pairs={{0,1},{1,2},{2,3},{3,4},{4,5},{5,6},{6,7},{7,8},{8,9},{9,10},{10,1... | collective-permute-start | bytes 1572872 | tf_op jit(solution)/shard_map/ppermute | solution.py:21
  26.1 11.5 %collective-permute-start.2 = (f32[1,2048]{1,0:T(1,128)S(1)}, f32[1,2048]{1,0:T(1,128)S(1)}, u32[]{:S(2)}, u32[]{:S(2)}) collective-permute-start(f32[1,2048]{1,0:T(1,128)S(1)} %slice.36), channel_id=1, source_target_pairs={{2,0},{3,1},{4,2},{5,3},{6,4},{7,5},{8,6},{9,7},{10,8},{11,9},{12,... | collective-permute-start | bytes 24584 | tf_op jit(solution)/shard_map/ppermute | solution.py:21
  55.0 16.1 %copy-start.1 = (bf16[1024,2048]{1,0:T(8,128)(2,1)S(1)}, bf16[1024,2048]{1,0:T(8,128)(2,1)}, u32[]{:S(2)}) copy-start(bf16[1024,2048]{1,0:T(8,128)(2,1)} %copy-done) | copy-start | bytes 12582916
  55.0 16.1 %copy-start.8 = (f32[256]{0:T(256)S(1)}, f32[256]{0:T(256)}, u32[]{:S(2)}) copy-start(f32[256]{0:T(256)} %param.16) | copy-start | bytes 3076
  71.1 15.7 %copy-start.3 = (f32[16,4,2048]{2,1,0:T(4,128)S(1)}, f32[16,4,2048]{2,1,0:T(4,128)}, u32[]{:S(2)}) copy-start(f32[16,4,2048]{2,1,0:T(4,128)} %log.1) | copy-start | bytes 1572868
  71.1 15.7 %copy-start.7 = (f32[16,256]{1,0:T(8,128)S(1)}, f32[16,256]{1,0:T(8,128)}, u32[]{:S(2)}) copy-start(f32[16,256]{1,0:T(8,128)} %subspace.1) | copy-start | bytes 49156
  73.4 1.2 %collective-permute-start.5 = (f32[32,256]{1,0:T(8,128)S(1)}, f32[32,256]{1,0:T(8,128)S(1)}, u32[]{:S(2)}, u32[]{:S(2)}) collective-permute-start(f32[32,256]{1,0:T(8,128)S(1)} %shard_map.107), channel_id=1, source_target_pairs={{0,1},{1,0},{2,3},{3,2},{4,5},{5,4},{6,7},{7,6},{8,9},{9,8},{10,11... | collective-permute-start | bytes 98312 | tf_op jit(solution)/shard_map/ppermute | solution.py:37
  74.6 5.0 %collective-permute-start.8 = (f32[32,256]{1,0:T(8,128)S(1)}, f32[32,256]{1,0:T(8,128)S(1)}, u32[]{:S(2)}, u32[]{:S(2)}) collective-permute-start(f32[32,256]{1,0:T(8,128)S(1)} %add.21), channel_id=1, source_target_pairs={{0,6},{1,7},{2,4},{3,5},{4,2},{5,3},{6,0},{7,1},{8,14},{9,15},{10,... | collective-permute-start | bytes 98312 | tf_op jit(solution)/shard_map/ppermute | solution.py:37
  75.2 4.4 %collective-permute-start.7 = (f32[32,256]{1,0:T(8,128)S(1)}, f32[32,256]{1,0:T(8,128)S(1)}, u32[]{:S(2)}, u32[]{:S(2)}) collective-permute-start(f32[32,256]{1,0:T(8,128)S(1)} %add.21), channel_id=1, source_target_pairs={{0,4},{1,5},{2,6},{3,7},{4,0},{5,1},{6,2},{7,3},{8,12},{9,13},{10,... | collective-permute-start | bytes 98312 | tf_op jit(solution)/shard_map/ppermute | solution.py:37
  76.5 3.9 %collective-permute-start.6 = (f32[32,256]{1,0:T(8,128)S(1)}, f32[32,256]{1,0:T(8,128)S(1)}, u32[]{:S(2)}, u32[]{:S(2)}) collective-permute-start(f32[32,256]{1,0:T(8,128)S(1)} %add.21), channel_id=1, source_target_pairs={{0,2},{1,3},{2,0},{3,1},{4,6},{5,7},{6,4},{7,5},{8,10},{9,11},{10,... | collective-permute-start | bytes 98312 | tf_op jit(solution)/shard_map/ppermute | solution.py:37
  80.5 5.8 %collective-permute-start.11 = (f32[32,256]{1,0:T(8,128)S(1)}, f32[32,256]{1,0:T(8,128)S(1)}, u32[]{:S(2)}, u32[]{:S(2)}) collective-permute-start(f32[32,256]{1,0:T(8,128)S(1)} %add_add_fusion.1), channel_id=1, source_target_pairs={{0,24},{1,25},{2,26},{3,27},{4,28},{5,29},{6,30},{7,31},{8,16},{9,... | collective-permute-start | bytes 98312 | tf_op jit(solution)/shard_map/ppermute | solution.py:37
  81.1 5.2 %collective-permute-start.10 = (f32[32,256]{1,0:T(8,128)S(1)}, f32[32,256]{1,0:T(8,128)S(1)}, u32[]{:S(2)}, u32[]{:S(2)}) collective-permute-start(f32[32,256]{1,0:T(8,128)S(1)} %add_add_fusion.1), channel_id=1, source_target_pairs={{0,16},{1,17},{2,18},{3,19},{4,20},{5,21},{6,22},{7,23},{8,24},{9,... | collective-permute-start | bytes 98312 | tf_op jit(solution)/shard_map/ppermute | solution.py:37
  82.6 4.2 %collective-permute-start.9 = (f32[32,256]{1,0:T(8,128)S(1)}, f32[32,256]{1,0:T(8,128)S(1)}, u32[]{:S(2)}, u32[]{:S(2)}) collective-permute-start(f32[32,256]{1,0:T(8,128)S(1)} %add_add_fusion.1), channel_id=1, source_target_pairs={{0,8},{1,9},{2,10},{3,11},{4,12},{5,13},{6,14},{7,15},{8,0},{9,1},... | collective-permute-start | bytes 98312 | tf_op jit(solution)/shard_map/ppermute | solution.py:37
